TPU v7x, 256 devices: a whole 4x4x8 slice. The times are simulated.
256 devices in a mesh: shuffle: 64 (over y, z, core), dp: 4 (over x).
Axes of the slice: x: 4, y: 4, z: 8, core: 2. Of those that a mesh axis runs over, the one named last changes fastest.
Arguments:
- fact_rows: bfloat16 [1048576, 512], P(('shuffle', 'dp')), may hold values from -6 to 6
- owner_index: int32 [1048576, 1], P(('shuffle', 'dp')), may hold values from 0 to 63, as said below
- light_slot: int32 [1048576, 1], P(('shuffle', 'dp')), may hold values from 0 to 1023
- heavy_flag: int32 [1048576, 1], P(('shuffle', 'dp')), may hold values from 0 to 1
- heavy_key: int32 [1048576, 1], P(('shuffle', 'dp')), may hold values from 0 to 1023
- light_dims: bfloat16 [65536, 512], P('shuffle', 'dp'), may hold values from -4 to 4
- heavy_dims: bfloat16 [1024, 512], P(('shuffle', 'dp')), may hold values from -1.5 to 1.5
Outputs:
- light_joined: bfloat16 [65536, 512], P('shuffle', 'dp')
- heavy_joined: bfloat16 [1024, 512], replicated
Inputs may be any that keep to these rules, and one draw needn't show every extreme that they name: `owner_index`: among the rows of one device at most 96 name the same owner, and in every draw some device has exactly 96 rows with heavy_flag 0 that name one owner.
All inputs are finite; a program needn't handle non-finite values.
Results may differ from a plain program's by a relative error of at most 0.001.
Values may be sent and summed in bfloat16 or wider, within the bound.
A program may use at most 64 MiB of HBM per device.

v0:
```python
import math

import jax
import jax.numpy as jnp
from jax import lax
from jax.sharding import Mesh
from jax.sharding import PartitionSpec as P

H = 1024
SLOTS = 1024
SHUFFLE = ("shuffle_0", "shuffle_1", "shuffle_2")
SHUFFLE_DP = ("shuffle_0", "shuffle_1", "shuffle_2", "dp")


def split_up(value, dim, count):
    dims = value.shape
    pieces = value.reshape(*dims[:dim], count, dims[dim] // count, *dims[dim + 1 :])
    return jnp.moveaxis(pieces, dim, 0)


def sum_at_owner(value, axis, dim):
    count = lax.axis_size(axis)
    pieces = lax.all_to_all(split_up(value, dim, count), axis, 0, 0, tiled=True)
    return jnp.sum(pieces, axis=0)


def summed_rows(value, axes, dim):
    far, near = axes
    pieces = split_up(value, dim, lax.axis_size(far))
    nearer = sum_at_owner(pieces, near, dim + 1)
    arrived = lax.all_to_all(nearer, far, split_axis=0, concat_axis=0, tiled=True)
    return arrived.sum(axis=0)


def aggregate(values, labels, label_count):
    block_size = math.gcd(label_count, 256)

    def pick_block(offset):
        onehot = (
            labels[:, None] == offset + jnp.arange(block_size, dtype=jnp.int32)[None, :]
        ).astype(jnp.bfloat16)
        return lax.dot_general(
            onehot, values, (((0,), (0,)), ((), ())), preferred_element_type=jnp.float32
        )

    offsets = jnp.arange(label_count // block_size, dtype=jnp.int32) * block_size
    blocks = lax.map(pick_block, offsets)
    return blocks.reshape(label_count, values.shape[1])


def bucket(values, target, groups, capacity):
    chosen = target >= 0
    owner_of = jnp.where(chosen, target // SLOTS, -1)
    slot_of = jnp.where(chosen, target % SLOTS, -1)
    onehot = (
        (owner_of[:, None] == jnp.arange(groups, dtype=jnp.int32)[None, :]) & chosen[:, None]
    ).astype(jnp.int32)
    position = jnp.sum((jnp.cumsum(onehot, axis=0) - 1) * onehot, axis=1)
    places = jnp.where(chosen, owner_of * capacity + position, groups * capacity)
    buffer = (
        jnp.zeros((groups * capacity, values.shape[1]), values.dtype)
        .at[places]
        .set(values, mode="drop")
    )
    slot_buffer = jnp.full((groups * capacity,), -1, jnp.int32).at[places].set(slot_of, mode="drop")
    return (
        buffer.reshape(groups, capacity, values.shape[1]),
        slot_buffer.reshape(groups, capacity),
    )


def shards(fact_rows, owner_index, light_slot, heavy_flag, heavy_key, light_dims, heavy_dims):
    rows_here = fact_rows.shape[0]
    groups = lax.axis_size(SHUFFLE)
    capacity = 3 * rows_here // (2 * groups)
    target = jnp.where(heavy_flag[:, 0] == 0, owner_index[:, 0] * SLOTS + light_slot[:, 0], -1)
    heavy_labels = jnp.where(heavy_flag[:, 0] == 1, heavy_key[:, 0], -1)
    partial_value = aggregate(fact_rows, heavy_labels, H)
    buffer, slot_buffer = bucket(fact_rows, target, groups, capacity)
    arrived, arrived_slots = (
        lax.all_to_all(buffer, SHUFFLE, split_axis=0, concat_axis=0, tiled=True),
        lax.all_to_all(slot_buffer, SHUFFLE, split_axis=0, concat_axis=0, tiled=True),
    )
    local_sums = aggregate(arrived.reshape(-1, arrived.shape[2]), arrived_slots.reshape(-1), SLOTS)
    totals = sum_at_owner(local_sums, "dp", 1)
    light_joined = (totals * light_dims.astype(jnp.float32)).astype(jnp.bfloat16)
    shares = summed_rows(partial_value, (("shuffle_0", "shuffle_1"), ("shuffle_2", "dp")), 0)
    joined_here = (shares * heavy_dims.astype(jnp.float32)).astype(jnp.bfloat16)
    heavy_joined = lax.all_gather(joined_here, SHUFFLE_DP, axis=0, tiled=True)
    return (light_joined, heavy_joined)


def solution(mesh):
    torus = Mesh(
        mesh.devices.reshape(4, 8, 2, mesh.shape["dp"]),
        ("shuffle_0", "shuffle_1", "shuffle_2", "dp"),
    )
    return jax.shard_map(
        shards,
        mesh=torus,
        in_specs=(
            P(SHUFFLE_DP, None),
            P(SHUFFLE_DP, None),
            P(SHUFFLE_DP, None),
            P(SHUFFLE_DP, None),
            P(SHUFFLE_DP, None),
            P(SHUFFLE, "dp"),
            P(SHUFFLE_DP, None),
        ),
        out_specs=(P(SHUFFLE, "dp"), P()),
        check_vma=False,
    )
```

profile of v0, /device:TPU:1, one launch (start us, length us, event | category | flops | bytes accessed | tf_op | source)
XLA Modules:
  0.0 374.1 jit_solution(15838419750780323920)
XLA Ops:
  7.2 0.8 compare_select_fusion.1
  7.9 0.2 broadcast.98.clone.1
  8.2 21.5 %while.21 = (s32[]{:T(128)}, f32[4,256,512]{2,1,0:T(8,128)S(1)}, s32[4096]{0:T(1024)S(1)}, s32[4]{0:T(128)S(1)}, bf16[4096,512]{1,0:T(8,128)(2,1)}, /*index=5*/s32[]{:T(128)}) while((s32[]{:T(128)}, f32[4,256,512]{2,1,0:T(8,128)S(1)}, s32[4096]{0:T(1024)S(1)}, s32[4]{0:T(128)S(1)}, bf16[4096,512]{1,0:T(8,128)(2,1)}, ...), condition=%wide.region_9.10_spmd, body=%wide.region_8.9_spmd.sunk | while | flops 1074790656 | bytes 4737113 | solution.py:47
  8.2 0.6 dynamic_slice.10
  8.8 0.6 iota_add_fusion.5
  9.5 4.1 %fusion.47 = f32[4,256,512]{2,1,0:T(8,128)S(1)} fusion(f32[4,256,512]{2,1,0:T(8,128)S(1)} %get-tuple-element.196, s32[]{:T(128)} %get-tuple-element.195, bf16[4096,512]{1,0:T(8,128)(2,1)} %get-tuple-element.205, s32[256]{0:T(256)S(1)} %iota_add_fusion.5, s32[4096]{0:T(1024)S(1)} %get-tuple-element.203), kind=kOutput, calls=%fused_computation.14.clone.1 | convolution fusion | flops 1074790400 | bytes 4736004 | tf_op jit(solution)/shard_map/while/body/eval_jaxpr/dot_general | solution.py:42
  13.6 0.6 dynamic_slice.10
  14.2 0.6 iota_add_fusion.5
  14.8 4.1 %fusion.47 = f32[4,256,512]{2,1,0:T(8,128)S(1)} fusion(f32[4,256,512]{2,1,0:T(8,128)S(1)} %get-tuple-element.196, s32[]{:T(128)} %get-tuple-element.195, bf16[4096,512]{1,0:T(8,128)(2,1)} %get-tuple-element.205, s32[256]{0:T(256)S(1)} %iota_add_fusion.5, s32[4096]{0:T(1024)S(1)} %get-tuple-element.203), kind=kOutput, calls=%fused_computation.14.clone.1 | convolution fusion | flops 1074790400 | bytes 4736004 | tf_op jit(solution)/shard_map/while/body/eval_jaxpr/dot_general | solution.py:42
  18.9 0.6 dynamic_slice.10
  19.5 0.6 iota_add_fusion.5
  20.2 4.1 %fusion.47 = f32[4,256,512]{2,1,0:T(8,128)S(1)} fusion(f32[4,256,512]{2,1,0:T(8,128)S(1)} %get-tuple-element.196, s32[]{:T(128)} %get-tuple-element.195, bf16[4096,512]{1,0:T(8,128)(2,1)} %get-tuple-element.205, s32[256]{0:T(256)S(1)} %iota_add_fusion.5, s32[4096]{0:T(1024)S(1)} %get-tuple-element.203), kind=kOutput, calls=%fused_computation.14.clone.1 | convolution fusion | flops 1074790400 | bytes 4736004 | tf_op jit(solution)/shard_map/while/body/eval_jaxpr/dot_general | solution.py:42
  24.3 0.6 dynamic_slice.10
  24.9 0.6 iota_add_fusion.5
  25.5 4.1 %fusion.47 = f32[4,256,512]{2,1,0:T(8,128)S(1)} fusion(f32[4,256,512]{2,1,0:T(8,128)S(1)} %get-tuple-element.196, s32[]{:T(128)} %get-tuple-element.195, bf16[4096,512]{1,0:T(8,128)(2,1)} %get-tuple-element.205, s32[256]{0:T(256)S(1)} %iota_add_fusion.5, s32[4096]{0:T(1024)S(1)} %get-tuple-element.203), kind=kOutput, calls=%fused_computation.14.clone.1 | convolution fusion | flops 1074790400 | bytes 4736004 | tf_op jit(solution)/shard_map/while/body/eval_jaxpr/dot_general | solution.py:42
  29.7 1.7 reshape_reshape_reshape.3
  31.3 3.4 copy.24
  34.7 6.7 %all-to-all-start.3 = ((f32[8,32,4,512]{3,2,1,0:T(4,128)}), f32[8,32,4,512]{3,2,1,0:T(4,128)S(1)}, u32[]{:S(2)}, u32[]{:S(2)}) async-start(f32[8,32,4,512]{3,2,1,0:T(4,128)} %copy.24), calls=%async_computation.3 | async-start | bytes 4194304 | tf_op jit(solution)/shard_map/all_to_all | solution.py:23
  41.4 0.1 fusion.32
  41.5 0.1 fusion.29
  41.6 1.1 fusion.26
  42.7 32.3 %reduce-window.6 = s32[64,32,128]{2,1,0:T(8,128)S(1)} reduce-window(s32[64,32,128]{2,1,0:T(8,128)} %fusion.26, s32[]{:T(128)} %copy.47), window={size=1x1x128 pad=0_0x0_0x127_0}, to_apply=%region_0.1 | reduce-window | flops 33292288 | bytes 2097156 | tf_op jit(solution)/shard_map/reduce-window
  75.1 1.3 slice.8
  76.4 1.7 copy.26
  78.0 0.2 reduce-window.9
  78.2 0.3 add_add_fusion
  78.6 0.9 fusion.23
  79.5 0.1 compare_select_fusion
  79.6 15.5 %scatter_custom_fusion = s32[6144]{0:T(1024)S(1)} fusion(s32[4096]{0:T(1024)S(1)} %bitcast.71, s32[4096]{0:T(1024)S(1)} %fusion.28, s32[]{:T(128)} %constant.57.clone.1), kind=kCustom, calls=%fused_computation.41 | custom fusion | bytes 24580 | tf_op jit(solution)/shard_map/scatter | solution.py:65
  95.2 0.7 all_to_all.20
  95.9 0.0 all-to-all-done.3
  95.9 10.8 %all-to-all-start = ((s32[64,1,96]{2,1,0:T(1,128)}), s32[64,1,96]{2,1,0:T(1,128)S(1)}, u32[]{:S(2)}, u32[]{:S(2)}) async-start(s32[64,1,96]{2,1,0:T(1,128)} %all_to_all.20), calls=%async_computation | async-start | bytes 65536 | tf_op jit(solution)/shard_map/all_to_all | solution.py:82
  106.7 1.1 reduce_sum.41
  107.9 8.1 %all-to-all-done = s32[64,1,96]{2,1,0:T(1,128)S(1)} async-done(((s32[64,1,96]{2,1,0:T(1,128)}), s32[64,1,96]{2,1,0:T(1,128)S(1)}, u32[]{:S(2)}, u32[]{:S(2)}) %all-to-all-start) | async-done | bytes 24608 | tf_op jit(solution)/shard_map/all_to_all | solution.py:82
  116.0 3.9 %all-to-all-start.4 = ((f32[32,4,512]{2,1,0:T(4,128)}), f32[32,4,512]{2,1,0:T(4,128)S(1)}, u32[]{:S(2)}, u32[]{:S(2)}) async-start(f32[32,4,512]{2,1,0:T(4,128)} %reduce_sum.41), calls=%async_computation.4 | async-start | bytes 524288 | tf_op jit(solution)/shard_map/all_to_all | solution.py:31
  119.9 22.4 %scatter_custom_fusion.1 = bf16[6144,512]{1,0:T(8,128)(2,1)} fusion(s32[4096]{0:T(1024)S(1)} %bitcast.72, bf16[4096,512]{1,0:T(8,128)(2,1)} %get-tuple-element.221, bf16[]{:T(256)} %constant.64.clone.1), kind=kCustom, calls=%fused_computation.16 | custom fusion | bytes 6291968 | tf_op jit(solution)/shard_map/scatter | solution.py:63
  142.3 10.9 %all-to-all-start.1 = ((bf16[64,96,512]{2,1,0:T(8,128)(2,1)}), bf16[64,96,512]{2,1,0:T(8,128)(2,1)}, u32[]{:S(2)}, u32[]{:S(2)}) async-start(bf16[64,96,512]{2,1,0:T(8,128)(2,1)} %bitcast.57), calls=%async_computation.1 | async-start | bytes 12582912 | tf_op jit(solution)/shard_map/all_to_all | solution.py:81
  153.2 0.0 all-gather.3.cloned.1.call-start
  153.3 0.1 eq.146
  153.4 0.1 reduce_sum.42
  153.4 0.6 fusion.33
  154.0 0.0 all-gather.3.cloned.1.call-update
  154.0 142.8 %all-to-all-done.1 = bf16[64,96,512]{2,1,0:T(8,128)(2,1)} async-done(((bf16[64,96,512]{2,1,0:T(8,128)(2,1)}), bf16[64,96,512]{2,1,0:T(8,128)(2,1)}, u32[]{:S(2)}, u32[]{:S(2)}) %all-to-all-start.1) | async-done | bytes 6291488 | tf_op jit(solution)/shard_map/all_to_all | solution.py:81
  296.9 0.2 broadcast.98.clone
  297.1 33.5 %while.22 = (s32[]{:T(128)}, f32[4,256,512]{2,1,0:T(8,128)S(1)}, s32[64,96]{1,0:T(8,128)}, s32[4]{0:T(128)S(1)}, bf16[6144,512]{1,0:T(8,128)(2,1)}, /*index=5*/s32[6144]{0:T(1024)S(1)}, s32[]{:T(128)}) while((s32[]{:T(128)}, f32[4,256,512]{2,1,0:T(8,128)S(1)}, s32[64,96]{1,0:T(8,128)}, s32[4]{0:T(128)S(1)}, ...), condition=%wide.wide.region_6.7_spmd, body=%wide.wide.region_5.6_spmd.sunk | while | flops 1612185856 | bytes 6842465 | solution.py:47
  297.1 0.6 dynamic_slice.11
  297.7 0.6 iota_add_fusion.6
  298.3 7.2 %fusion.50 = f32[4,256,512]{2,1,0:T(8,128)S(1)} fusion(f32[4,256,512]{2,1,0:T(8,128)S(1)} %get-tuple-element.176, s32[]{:T(128)} %get-tuple-element.175, bf16[6144,512]{1,0:T(8,128)(2,1)} %get-tuple-element.186, s32[256]{0:T(256)S(1)} %iota_add_fusion.6, s32[6144]{0:T(1024)S(1)} %get-tuple-element.187), kind=kOutput, calls=%fused_computation.7.clone.clone.1 | convolution fusion | flops 1612185600 | bytes 6841348 | tf_op jit(solution)/shard_map/while/body/eval_jaxpr/dot_general | solution.py:42
  305.5 0.6 dynamic_slice.11
  306.1 0.6 iota_add_fusion.6
  306.7 7.2 %fusion.50 = f32[4,256,512]{2,1,0:T(8,128)S(1)} fusion(f32[4,256,512]{2,1,0:T(8,128)S(1)} %get-tuple-element.176, s32[]{:T(128)} %get-tuple-element.175, bf16[6144,512]{1,0:T(8,128)(2,1)} %get-tuple-element.186, s32[256]{0:T(256)S(1)} %iota_add_fusion.6, s32[6144]{0:T(1024)S(1)} %get-tuple-element.187), kind=kOutput, calls=%fused_computation.7.clone.clone.1 | convolution fusion | flops 1612185600 | bytes 6841348 | tf_op jit(solution)/shard_map/while/body/eval_jaxpr/dot_general | solution.py:42
  313.9 0.6 dynamic_slice.11
  314.5 0.6 iota_add_fusion.6
  315.1 7.2 %fusion.50 = f32[4,256,512]{2,1,0:T(8,128)S(1)} fusion(f32[4,256,512]{2,1,0:T(8,128)S(1)} %get-tuple-element.176, s32[]{:T(128)} %get-tuple-element.175, bf16[6144,512]{1,0:T(8,128)(2,1)} %get-tuple-element.186, s32[256]{0:T(256)S(1)} %iota_add_fusion.6, s32[6144]{0:T(1024)S(1)} %get-tuple-element.187), kind=kOutput, calls=%fused_computation.7.clone.clone.1 | convolution fusion | flops 1612185600 | bytes 6841348 | tf_op jit(solution)/shard_map/while/body/eval_jaxpr/dot_general | solution.py:42
  322.3 0.6 dynamic_slice.11
  322.9 0.6 iota_add_fusion.6
  323.5 7.2 %fusion.50 = f32[4,256,512]{2,1,0:T(8,128)S(1)} fusion(f32[4,256,512]{2,1,0:T(8,128)S(1)} %get-tuple-element.176, s32[]{:T(128)} %get-tuple-element.175, bf16[6144,512]{1,0:T(8,128)(2,1)} %get-tuple-element.186, s32[256]{0:T(256)S(1)} %iota_add_fusion.6, s32[6144]{0:T(1024)S(1)} %get-tuple-element.187), kind=kOutput, calls=%fused_computation.7.clone.clone.1 | convolution fusion | flops 1612185600 | bytes 6841348 | tf_op jit(solution)/shard_map/while/body/eval_jaxpr/dot_general | solution.py:42
  330.7 1.7 reshape_reshape.3
  332.4 3.1 copy.23
  335.5 4.5 %all-to-all-start.2 = ((f32[4,1024,128]{2,1,0:T(8,128)}), f32[4,1024,128]{2,1,0:T(8,128)S(1)}, u32[]{:S(2)}, u32[]{:S(2)}) async-start(f32[4,1024,128]{2,1,0:T(8,128)} %copy.23), calls=%async_computation.2 | async-start | bytes 4194304 | tf_op jit(solution)/shard_map/all_to_all | solution.py:23
  340.0 2.1 reshape.81
  342.2 24.2 %all-to-all-done.2 = f32[4,1024,128]{2,1,0:T(8,128)S(1)} async-done(((f32[4,1024,128]{2,1,0:T(8,128)}), f32[4,1024,128]{2,1,0:T(8,128)S(1)}, u32[]{:S(2)}, u32[]{:S(2)}) %all-to-all-start.2) | async-done | bytes 2097184 | tf_op jit(solution)/shard_map/all_to_all | solution.py:23
  366.3 0.1 reduce_sum.40
  366.5 0.8 multiply_convert_fusion
  (16 shorter events, 0.0 us)
Async XLA Ops:
  31.3 10.1 %copy-start.2 = (s32[4096,1]{0,1:T(1,128)S(1)}, s32[4096,1]{0,1:T(1,128)}, u32[]{:S(2)}) copy-start(s32[4096,1]{0,1:T(1,128)} %param.14) | copy-start | bytes 49156
  31.3 10.1 %copy-start.3 = (s32[4096,1]{0,1:T(1,128)S(1)}, s32[4096,1]{0,1:T(1,128)}, u32[]{:S(2)}) copy-start(s32[4096,1]{0,1:T(1,128)} %param.13) | copy-start | bytes 49156
  31.3 10.1 %copy-start.4 = (s32[4096,1]{0,1:T(1,128)S(1)}, s32[4096,1]{0,1:T(1,128)}, u32[]{:S(2)}) copy-start(s32[4096,1]{0,1:T(1,128)} %param.12) | copy-start | bytes 49156
  34.7 61.2 %all-to-all-start.3 = ((f32[8,32,4,512]{3,2,1,0:T(4,128)}), f32[8,32,4,512]{3,2,1,0:T(4,128)S(1)}, u32[]{:S(2)}, u32[]{:S(2)}) async-start(f32[8,32,4,512]{3,2,1,0:T(4,128)} %copy.24), calls=%async_computation.3 | async-start | bytes 4194304 | tf_op jit(solution)/shard_map/all_to_all | solution.py:23
  95.9 20.1 %all-to-all-start = ((s32[64,1,96]{2,1,0:T(1,128)}), s32[64,1,96]{2,1,0:T(1,128)S(1)}, u32[]{:S(2)}, u32[]{:S(2)}) async-start(s32[64,1,96]{2,1,0:T(1,128)} %all_to_all.20), calls=%async_computation | async-start | bytes 65536 | tf_op jit(solution)/shard_map/all_to_all | solution.py:82
  116.0 37.3 %copy-start.1 = (s32[64,1,96]{2,1,0:T(1,128)}, s32[64,1,96]{2,1,0:T(1,128)S(1)}, u32[]{:S(2)}) copy-start(s32[64,1,96]{2,1,0:T(1,128)S(1)} %all-to-all-done) | copy-start | bytes 73732
  116.0 26.3 %all-to-all-start.4 = ((f32[32,4,512]{2,1,0:T(4,128)}), f32[32,4,512]{2,1,0:T(4,128)S(1)}, u32[]{:S(2)}, u32[]{:S(2)}) async-start(f32[32,4,512]{2,1,0:T(4,128)} %reduce_sum.41), calls=%async_computation.4 | async-start | bytes 524288 | tf_op jit(solution)/shard_map/all_to_all | solution.py:31
  142.3 11.1 %copy-start.5 = (bf16[4,512]{1,0:T(4,128)(2,1)S(1)}, bf16[4,512]{1,0:T(4,128)(2,1)}, u32[]{:S(2)}) copy-start(bf16[4,512]{1,0:T(4,128)(2,1)} %param.17) | copy-start | bytes 12292
  142.3 154.6 %all-to-all-start.1 = ((bf16[64,96,512]{2,1,0:T(8,128)(2,1)}), bf16[64,96,512]{2,1,0:T(8,128)(2,1)}, u32[]{:S(2)}, u32[]{:S(2)}) async-start(bf16[64,96,512]{2,1,0:T(8,128)(2,1)} %bitcast.57), calls=%async_computation.1 | async-start | bytes 12582912 | tf_op jit(solution)/shard_map/all_to_all | solution.py:81
  153.2 186.8 %all-gather.3.cloned.1.call-start = ((), (), s32[]{:S(2)}) async-start(), calls=%async_computation.5 | async-start | bytes 1052672 | tf_op jit(solution)/shard_map/all_gather | solution.py:89
  335.5 31.0 %copy-start = (bf16[1024,128]{1,0:T(8,128)(2,1)S(1)}, bf16[1024,128]{1,0:T(8,128)(2,1)}, u32[]{:S(2)}) copy-start(bf16[1024,128]{1,0:T(8,128)(2,1)} %param.16) | copy-start | bytes 786436
  335.5 30.8 %all-to-all-start.2 = ((f32[4,1024,128]{2,1,0:T(8,128)}), f32[4,1024,128]{2,1,0:T(8,128)S(1)}, u32[]{:S(2)}, u32[]{:S(2)}) async-start(f32[4,1024,128]{2,1,0:T(8,128)} %copy.23), calls=%async_computation.2 | async-start | bytes 4194304 | tf_op jit(solution)/shard_map/all_to_all | solution.py:23
Sparse Core Ops, SparseCore 0:
  158.3 124.1 all-gather.2
where the time goes:
time: 378 us; the launch traced here: 374 us
  waiting for transfers between devices  175 us (46%)
  local copies, waits for them, and re-layouts  58.9 us (16%)
  matrix products  45.2 us (12%)
  other arithmetic  43.5 us (12%)
  starting transfers between devices  36.9 us (10%)
  between operations  14.2 us (4%)
    all_to_all x1, waiting for transfers between devices, shards(): lax.all_to_all(buffer, SHUFFLE, split_axis=0, concat_axis=0, tiled=True)  143 us
    dot_general x8, matrix products, pick_block(): lax.dot_general(onehot, values, (((0,), (0,)), ((), ())), preferred_eleme...  45.2 us
    another operation x2, other arithmetic  32.5 us
    all_to_all x2, waiting for transfers between devices, sum_at_owner(): pieces = lax.all_to_all(split_up(value, dim, count), axis, 0, 0, tiled=True)  24.2 us
    scatter x1, local copies, waits for them, and re-layouts, bucket(): buffer = jnp.zeros((groups * capacity, values.shape[1]), values.dtype).at...  22.4 us
    scatter x1, local copies, waits for them, and re-layouts, bucket(): jnp.full((groups * capacity,), -1, jnp.int32).at[places]  15.5 us
    all_to_all x2, starting transfers between devices, sum_at_owner(): pieces = lax.all_to_all(split_up(value, dim, count), axis, 0, 0, tiled=True)  11.3 us
    all_to_all x1, starting transfers between devices, shards(): lax.all_to_all(buffer, SHUFFLE, split_axis=0, concat_axis=0, tiled=True)  10.9 us
  transfers between devices with their start and end apart: 6, of which 3 were waited for; matrix products, arithmetic and copies ran while one was open for 32% of the time, Pallas kernels for 0%

commit v1 on v0

v1 whole, which is shorter than its diff:
```python
import functools

import jax
import jax.numpy as jnp
from jax import lax
from jax.experimental import pallas as pl
from jax.experimental.pallas import tpu as pltpu
from jax.sharding import Mesh
from jax.sharding import PartitionSpec as P

ROWS = 4096
F = 512
H = 1024
SLOTS = 1024
CAP = 96
NY, NZ, NC, NX = 4, 8, 2, 4
OWNERS = NY * NZ * NC
SHUFFLE = ("y", "z", "c")
ALL = ("y", "z", "c", "x")
LANES = 128
BLOCKS = ROWS // LANES


def table_kernel(owner_ref, slot_ref, flag_ref, source_ref, key_ref):
    row = lax.broadcasted_iota(jnp.int32, (LANES, 2 * LANES), 0)
    col = lax.broadcasted_iota(jnp.int32, (LANES, 2 * LANES), 1)
    before = jnp.where((row < col) | (col >= LANES), 1.0, 0.0).astype(jnp.bfloat16)
    owner_of = lax.broadcasted_iota(jnp.int32, (OWNERS, LANES), 0)
    rank_of = lax.broadcasted_iota(jnp.int32, (LANES, LANES), 0).astype(jnp.float32)
    lane = lax.broadcasted_iota(jnp.int32, (1, LANES), 1)

    def step(b, carried):
        seen, table = carried
        here = pl.ds(b, 1)
        owner = jnp.where(flag_ref[here, :] == 0, owner_ref[here, :], -1)
        slot = slot_ref[here, :]
        hot = jnp.where(owner_of == owner, 1.0, 0.0)
        hot16 = hot.astype(jnp.bfloat16)
        counts = jnp.dot(hot16, before, preferred_element_type=jnp.float32)
        rank = jnp.sum(hot * (counts[:, :LANES] + seen), axis=0, keepdims=True)
        at_rank = rank_of == rank
        high = lax.shift_right_logical(slot, 8)
        values = (lane + 1, jnp.full((1, LANES), b, jnp.int32), slot - high * 256, high)
        placed = jnp.concatenate(
            [jnp.where(at_rank, value.astype(jnp.float32), 0.0) for value in values], axis=0
        ).astype(jnp.bfloat16)
        found = lax.dot_general(
            hot16, placed, (((1,), (1,)), ((), ())), preferred_element_type=jnp.float32
        )
        return seen + counts[:, LANES:], table + found

    start = (jnp.zeros((OWNERS, LANES), jnp.float32), jnp.zeros((OWNERS, 4 * LANES), jnp.float32))
    _, table = lax.fori_loop(0, BLOCKS, step, start)
    first, block, low, high = (
        table[:, i * LANES : (i + 1) * LANES].astype(jnp.int32) for i in range(4)
    )
    filled = first > 0
    source_ref[...] = jnp.where(filled, (block * LANES + first - 1) * 4, 0)
    key_ref[...] = jnp.where(filled, high * 256 + low, -1)


def tables(owner, slot, flag):
    shape = jax.ShapeDtypeStruct((OWNERS, LANES), jnp.int32)
    return pl.pallas_call(table_kernel, out_shape=(shape, shape), name="tables")(owner, slot, flag)


def heavy_kernel(key_ref, flag_ref, x_ref, out_ref):
    step = pl.program_id(0)
    keys = lax.broadcasted_iota(jnp.int32, (H, LANES), 0)
    total = None
    for b in range(4):
        here = pl.ds(b, 1)
        key = jnp.where(flag_ref[here, :] == 1, key_ref[here, :], -1)
        hot = jnp.where(keys == key, 1.0, 0.0).astype(jnp.bfloat16)
        part = jnp.dot(
            hot, x_ref[b * LANES : (b + 1) * LANES, :], preferred_element_type=jnp.float32
        )
        total = part if total is None else total + part

    @pl.when(step == 0)
    def _():
        out_ref[...] = total

    @pl.when(step > 0)
    def _():
        out_ref[...] += total


def heavy_partial(key, flag, rows):
    steps = BLOCKS // 4
    return pl.pallas_call(
        heavy_kernel,
        grid=(steps,),
        in_specs=[
            pl.BlockSpec((None, 4, LANES), lambda i: (i, 0, 0)),
            pl.BlockSpec((None, 4, LANES), lambda i: (i, 0, 0)),
            pl.BlockSpec((4 * LANES, F), lambda i: (i, 0)),
        ],
        out_specs=pl.BlockSpec((H, F), lambda i: (0, 0)),
        out_shape=jax.ShapeDtypeStruct((H, F), jnp.float32),
        name="heavy_partial",
        cost_estimate=pl.CostEstimate(flops=2 * H * ROWS * F, bytes_accessed=6 << 20, transcendentals=0),
    )(key.reshape(steps, 4, LANES), flag.reshape(steps, 4, LANES), rows)


def gather_kernel(source_ref, x_ref, out_ref, wide, picked):
    z = pl.program_id(0)

    @pl.when(z == 0)
    def _():
        def widen(i, _):
            part = x_ref[pl.ds(pl.multiple_of(i * 64, 64), 64), :]
            for f in range(4):
                wide[pl.ds(i * 256 + f, 64, stride=4), :] = part[
                    :, f * LANES : (f + 1) * LANES
                ].astype(jnp.float32)
            return 0

        lax.fori_loop(0, ROWS // 64, widen, 0)

    for yc in range(8):
        owner = (yc // 2 * NZ + z) * 2 + yc % 2

        def pick(i, _):
            for k in range(16):
                r = i * 16 + k
                start = pl.multiple_of(source_ref[owner, r], 4)
                picked[pl.ds(pl.multiple_of((yc * CAP + r) * 4, 4), 4), :] = wide[pl.ds(start, 4), :]
            return 0

        lax.fori_loop(0, CAP // 16, pick, 0)
    for yc in range(8):
        for f in range(4):
            out_ref[f, yc, 0] = picked[pl.ds(yc * CAP * 4 + f, CAP, stride=4), :].astype(jnp.bfloat16)


def gather(source, rows):
    return pl.pallas_call(
        gather_kernel,
        grid_spec=pltpu.PrefetchScalarGridSpec(
            num_scalar_prefetch=1,
            grid=(NZ,),
            in_specs=[pl.BlockSpec((ROWS, F), lambda z, s: (0, 0))],
            out_specs=pl.BlockSpec((4, 8, 1, CAP, LANES), lambda z, s: (0, 0, z, 0, 0)),
            scratch_shapes=[
                pltpu.VMEM((ROWS * 4, LANES), jnp.float32),
                pltpu.VMEM((8 * CAP * 4, LANES), jnp.float32),
            ],
        ),
        out_shape=jax.ShapeDtypeStruct((4, 8, NZ, CAP, LANES), jnp.bfloat16),
        compiler_params=pltpu.CompilerParams(vmem_limit_bytes=60 << 20),
        name="gather_rows",
    )(source, rows)


def light_kernel(key_ref, rows_ref, out_ref):
    keys = lax.broadcasted_iota(jnp.int32, (SLOTS, LANES), 0)
    out_ref[...] = jnp.zeros_like(out_ref)

    def step(k, _):
        lanes = key_ref[0, pl.ds(k, 1), :]
        hot = jnp.where(keys == lanes, 1.0, 0.0).astype(jnp.bfloat16)
        part = rows_ref[0, pl.ds(pl.multiple_of(k * LANES, LANES), LANES), :]
        out_ref[0] += jnp.dot(hot, part, preferred_element_type=jnp.float32)
        return 0

    lax.fori_loop(0, 24, step, 0)


def light_partial(keys, rows):
    return pl.pallas_call(
        light_kernel,
        grid=(NZ,),
        in_specs=[
            pl.BlockSpec((1, 24, LANES), lambda z: (z, 0, 0)),
            pl.BlockSpec((1, 3072, LANES), lambda z: (z, 0, 0)),
        ],
        out_specs=pl.BlockSpec((1, SLOTS, LANES), lambda z: (z, 0, 0)),
        out_shape=jax.ShapeDtypeStruct((NZ, SLOTS, LANES), jnp.float32),
        name="light_partial",
    )(keys, rows)


def shards(rows, owner, slot, flag, heavy_key, light_dims, heavy_dims):
    lane_major = (BLOCKS, LANES)
    owner, slot, flag, heavy_key = (
        value.reshape(lane_major) for value in (owner, slot, flag, heavy_key)
    )
    source, key = tables(owner, slot, flag)
    heavy = heavy_partial(heavy_key, flag, rows)
    buckets = gather(source, rows)
    plane = ("x", "y", "c")
    sent = buckets.reshape(32, NZ * CAP, LANES)
    by_owner = key[:, :CAP].reshape(NY, NZ, NC, CAP).transpose(0, 2, 1, 3).reshape(8, NZ * CAP)
    sent_keys = jnp.broadcast_to(by_owner[None], (4, 8, NZ * CAP)).reshape(32, NZ * CAP)
    came_keys = lax.all_to_all(sent_keys, plane, 0, 0, tiled=True)
    came = lax.all_to_all(sent, plane, 0, 0, tiled=True)
    came = came.reshape(32, NZ, CAP, LANES).transpose(1, 0, 2, 3).reshape(NZ, 32 * CAP, LANES)
    came_keys = came_keys.reshape(32, NZ, CAP).transpose(1, 0, 2).reshape(NZ, 24, LANES)
    partial = light_partial(came_keys, came)
    totals = lax.psum_scatter(partial, "z", scatter_dimension=0, tiled=True)[0]
    light_joined = (totals * light_dims.astype(jnp.float32)).astype(jnp.bfloat16)
    every_dims = lax.all_gather(heavy_dims, ALL, axis=0, tiled=True)
    heavy_sums = lax.psum(heavy, ALL)
    heavy_joined = (heavy_sums * every_dims.astype(jnp.float32)).astype(jnp.bfloat16)
    return light_joined, heavy_joined


def solution(mesh):
    torus = Mesh(mesh.devices.reshape(NY, NZ, NC, NX), ALL)
    rows = P(ALL, None)
    return jax.shard_map(
        shards,
        mesh=torus,
        in_specs=(rows, rows, rows, rows, rows, P(SHUFFLE, "x"), rows),
        out_specs=(P(SHUFFLE, "x"), P()),
        check_vma=False,
    )
```

time: 378 us -> 488 us (1.29)
  waiting for transfers between devices: 175 us -> 348 us
  Pallas kernels: 0 us -> 91 us
  local copies, waits for them, and re-layouts: 58.9 us -> 10.5 us
  matrix products: 45.2 us -> 0 us
  other arithmetic: 43.5 us -> 4.94 us
  starting transfers between devices: 36.9 us -> 16.1 us
    psum x0 -> x1, waiting for transfers between devices: none -> 286 us  [shards(): heavy_sums = lax.psum(heavy, ALL)]
    all_to_all x5 -> x2, waiting for transfers between devices: 175 us -> 61.7 us  [the longest x1 61.7 us: shards(): came = lax.all_to_all(sent, plane, 0, 0, tiled=True)]
    pallas_call x0 -> x4, Pallas kernels: none -> 91 us  [the longest x1 44.3 us: light_partial(): pl.pallas_call(light_kernel, grid=(NZ,), in_specs=[pl.BlockSpec((1, 24, L...]
    dot_general x8 -> x0, matrix products: 45.2 us -> none  [pick_block(): lax.dot_general(onehot, values, (((0,), (0,)), ((), ())), preferred_eleme...]
    scatter x2 -> x0, local copies, waits for them, and re-layouts: 38 us -> none  [the longest x1 22.4 us: bucket(): buffer = jnp.zeros((groups * capacity, values.shape[1]), values.dtype).at...]
    another operation x2 -> x0, other arithmetic: 32.5 us -> none
    all_to_all x5 -> x2, starting transfers between devices: 36.9 us -> 16 us  [the longest x1 8.57 us: shards(): came_keys = lax.all_to_all(sent_keys, plane, 0, 0, tiled=True)]
    another operation x5 -> x0, local copies, waits for them, and re-layouts: 5.56 us -> none  [the longest x2 3.41 us: split_up(): value.reshape(*dims[:dim], count, dims[dim] // count, *dims[dim + 1:])]
  transfers between devices with their start and end apart: 6 -> 5, of which waited for: 3 -> 2; matrix products, arithmetic and copies ran while one was open for 32% -> 2% of each run, Pallas kernels for 0% -> 16%
where the time goes in v1:
time: 488 us; the launch traced here: 486 us
  waiting for transfers between devices  348 us (71%)
  Pallas kernels  91 us (19%)
  starting transfers between devices  16.1 us (3%)
  between operations  15.5 us (3%)
  local copies, waits for them, and re-layouts  10.5 us (2%)
  other arithmetic  4.94 us (1%)
    psum x1, waiting for transfers between devices, shards(): heavy_sums = lax.psum(heavy, ALL)  286 us
    all_to_all x1, waiting for transfers between devices, shards(): came = lax.all_to_all(sent, plane, 0, 0, tiled=True)  61.7 us
    pallas_call x1, Pallas kernels, light_partial(): pl.pallas_call(light_kernel, grid=(NZ,), in_specs=[pl.BlockSpec((1, 24, L...  44.3 us
    pallas_call x1, Pallas kernels, gather(): pl.pallas_call(gather_kernel, grid_spec=pltpu.PrefetchScalarGridSpec(num_...  21.1 us
    pallas_call x1, Pallas kernels, heavy_partial(): pl.pallas_call(heavy_kernel, grid=(steps,), in_specs=[pl.BlockSpec((None,...  13.7 us
    pallas_call x1, Pallas kernels, tables(): pl.pallas_call(table_kernel, out_shape=(shape, shape), name='tables')  11.9 us
  transfers between devices with their start and end apart: 5, of which 2 were waited for; matrix products, arithmetic and copies ran while one was open for 2% of the time, Pallas kernels for 16%

profile of v1, /device:TPU:1, one launch (start us, length us, event | category | flops | bytes accessed | tf_op | source)
XLA Modules:
  0.0 486.3 jit_solution(17601188522577694847)
XLA Ops:
  8.0 11.9 %tables.1 = (s32[64,128]{1,0:T(8,128)}, s32[64,128]{1,0:T(8,128)}) custom-call(s32[32,128]{1,0:T(8,128)} %bitcast.28, s32[32,128]{1,0:T(8,128)} %bitcast.29, s32[32,128]{1,0:T(8,128)} %bitcast.30), custom_call_target="tpu_custom_call" | custom-call | tf_op jit(solution)/shard_map/tables/pallas_call | solution.py:64
  19.8 0.8 copy.16
  20.6 0.1 broadcast_in_dim.7
  20.7 0.7 all_to_all.9
  21.4 8.6 %all-to-all-start = ((s32[32,1,768]{2,1,0:T(1,128)}), s32[32,1,768]{2,1,0:T(1,128)S(1)}, u32[]{:S(2)}, u32[]{:S(2)}) async-start(s32[32,1,768]{2,1,0:T(1,128)} %all_to_all.9), calls=%async_computation | async-start | bytes 196608 | tf_op jit(solution)/shard_map/all_to_all | solution.py:196
  30.0 21.1 %gather_rows.1 = bf16[4,8,8,96,128]{4,3,2,1,0:T(8,128)(2,1)} custom-call(s32[64,128]{1,0:T(8,128)} %get-tuple-element.5.source_ref, bf16[4096,512]{1,0:T(8,128)(2,1)} %x_ref.3), custom_call_target="tpu_custom_call" | custom-call | tf_op jit(solution)/shard_map/gather_rows/pallas_call | solution.py:138
  51.1 0.0 all-to-all-done
  51.1 7.4 %all-to-all-start.1 = ((bf16[32,768,128]{2,1,0:T(8,128)(2,1)}), bf16[32,768,128]{2,1,0:T(8,128)(2,1)}, u32[]{:S(2)}, u32[]{:S(2)}) async-start(bf16[32,768,128]{2,1,0:T(8,128)(2,1)} %bitcast.23), calls=%async_computation.1 | async-start | bytes 12582912 | tf_op jit(solution)/shard_map/all_to_all | solution.py:197
  58.5 0.0 all-gather.3.cloned.1.call-start
  58.6 0.7 all-gather.3.cloned.1.call-update
  59.3 0.0 all-reduce.2.cloned.1.call-start
  59.3 13.7 %heavy_partial.1 = f32[1024,512]{1,0:T(8,128)} custom-call(s32[8,4,128]{2,1,0:T(4,128)} %bitcast.33, s32[8,4,128]{2,1,0:T(4,128)} %bitcast.31, bf16[4096,512]{1,0:T(8,128)(2,1)} %x_ref.3), custom_call_target="tpu_custom_call" | custom-call | flops 4294967296 | bytes 6291456 | tf_op jit(solution)/shard_map/heavy_partial/pallas_call | solution.py:91
  73.1 0.0 all-reduce.2.cloned.1.call-update
  73.1 0.0 reduce-scatter.2.cloned.1.call-start
  73.1 0.2 reduce
  73.4 0.1 reshape.41
  73.5 0.8 reshape.42.key_ref
  74.3 61.7 %all-to-all-done.1 = bf16[32,768,128]{2,1,0:T(8,128)(2,1)} async-done(((bf16[32,768,128]{2,1,0:T(8,128)(2,1)}), bf16[32,768,128]{2,1,0:T(8,128)(2,1)}, u32[]{:S(2)}, u32[]{:S(2)}) %all-to-all-start.1) | async-done | bytes 6291488 | tf_op jit(solution)/shard_map/all_to_all | solution.py:197
  136.0 6.8 %copy.14 = bf16[8,32,96,128]{3,2,1,0:T(8,128)(2,1)} copy(bf16[8,32,96,128]{3,2,0,1:T(8,128)(2,1)} %bitcast.8) | data formatting | bytes 12582912 | tf_op jit(solution)/shard_map/transpose | solution.py:198
  142.7 44.3 %light_partial.1 = f32[8,1024,128]{2,1,0:T(8,128)} custom-call(s32[8,24,128]{2,1,0:T(8,128)} %reshape.42.key_ref, bf16[8,3072,128]{2,1,0:T(8,128)(2,1)} %bitcast.24), custom_call_target="tpu_custom_call" | custom-call | tf_op jit(solution)/shard_map/light_partial/pallas_call | solution.py:171
  187.1 0.0 reduce-scatter.2.cloned.1.call-update
  187.1 0.0 all-gather.3.cloned.1.call-done
  187.1 1.3 reshape.48
  188.4 0.0 copy-start
  188.4 285.7 %all-reduce.2.cloned.1.call-done = f32[1024,512]{1,0:T(8,128)} async-done(((f32[1024,512]{1,0:T(8,128)}), f32[1024,512]{1,0:T(8,128)}) %all-reduce.2.cloned.1.call-update) | async-done | bytes 2097168 | tf_op jit(solution)/shard_map/psum | solution.py:204
  474.2 2.9 multiply_convert_fusion
  477.1 0.0 reduce-scatter.2.cloned.1.call-done
  477.1 0.0 copy-done
  477.1 1.8 fusion
  (2 shorter events, 0.0 us)
Async XLA Ops:
  21.4 29.7 %all-to-all-start = ((s32[32,1,768]{2,1,0:T(1,128)}), s32[32,1,768]{2,1,0:T(1,128)S(1)}, u32[]{:S(2)}, u32[]{:S(2)}) async-start(s32[32,1,768]{2,1,0:T(1,128)} %all_to_all.9), calls=%async_computation | async-start | bytes 196608 | tf_op jit(solution)/shard_map/all_to_all | solution.py:196
  51.1 84.9 %all-to-all-start.1 = ((bf16[32,768,128]{2,1,0:T(8,128)(2,1)}), bf16[32,768,128]{2,1,0:T(8,128)(2,1)}, u32[]{:S(2)}, u32[]{:S(2)}) async-start(bf16[32,768,128]{2,1,0:T(8,128)(2,1)} %bitcast.23), calls=%async_computation.1 | async-start | bytes 12582912 | tf_op jit(solution)/shard_map/all_to_all | solution.py:197
  58.5 128.6 %all-gather.3.cloned.1.call-start = ((), (), s32[]{:S(2)}) async-start(), calls=%async_computation.5 | async-start | bytes 1052672 | tf_op jit(solution)/shard_map/all_gather | solution.py:203
  59.3 414.9 %all-reduce.2.cloned.1.call-start = ((), (), s32[]{:S(2)}) async-start(), calls=%async_computation.4 | async-start | bytes 4194304 | tf_op jit(solution)/shard_map/psum | solution.py:204
  73.1 404.0 %reduce-scatter.2.cloned.1.call-start = ((), (), s32[]{:S(2)}) async-start(), calls=%async_computation.3 | async-start | bytes 4718592 | tf_op jit(solution)/shard_map/reduce_scatter | solution.py:201
  188.4 288.7 %copy-start = (bf16[1024,128]{1,0:T(8,128)(2,1)S(1)}, bf16[1024,128]{1,0:T(8,128)(2,1)}, u32[]{:S(2)}) copy-start(bf16[1024,128]{1,0:T(8,128)(2,1)} %param.12) | copy-start | bytes 786436
Sparse Core Ops, SparseCore 0:
  63.1 123.6 all-gather.2
  192.1 281.9 all-reduce.1
Sparse Core Ops, SparseCore 1:
  187.2 67.7 reduce-scatter.1

commit v2 on v0

v2 whole, which is shorter than its diff:
```python
import functools

import jax
import jax.numpy as jnp
from jax import lax
from jax.experimental import pallas as pl
from jax.experimental.pallas import tpu as pltpu
from jax.sharding import Mesh
from jax.sharding import PartitionSpec as P

ROWS = 4096
F = 512
H = 1024
SLOTS = 1024
CAP = 96
NY, NZ, NC, NX = 4, 8, 2, 4
OWNERS = NY * NZ * NC
SHUFFLE = ("y", "z", "c")
ALL = ("y", "z", "c", "x")
LANES = 128
PLANE = NX * NY * NC
MESH = pl.DeviceIdType.MESH
FAR_FIRST = (4, 3, -3, 2, -2, 1, -1, 0)
HALF = SLOTS // 2


def table_kernel(owner_ref, slot_ref, flag_ref, source_ref, key_ref):
    K = 2 * LANES
    row = lax.broadcasted_iota(jnp.int32, (K, K), 0)
    col = lax.broadcasted_iota(jnp.int32, (K, K), 1)
    before = jnp.where(row < col, 1.0, 0.0).astype(jnp.bfloat16)
    owner_of = lax.broadcasted_iota(jnp.int32, (OWNERS, K), 0)
    rank_of = lax.broadcasted_iota(jnp.int32, (CAP, K), 0).astype(jnp.float32)
    lane = lax.broadcasted_iota(jnp.int32, (1, K), 1)
    ones = jnp.ones((K, LANES), jnp.bfloat16)
    seen = jnp.zeros((OWNERS, 1), jnp.float32)
    table = jnp.zeros((4 * CAP, OWNERS), jnp.float32)
    for b in range(ROWS // K):
        owner = owner_ref[b : b + 1, :]
        owner = (owner >> 4) * 16 + (owner & 1) * 8 + ((owner >> 1) & 7)
        owner = jnp.where(flag_ref[b : b + 1, :] == 0, owner, -1)
        slot = slot_ref[b : b + 1, :]
        hot = jnp.where(owner_of == owner, 1.0, 0.0)
        hot16 = hot.astype(jnp.bfloat16)
        counts = jnp.dot(hot16, before, preferred_element_type=jnp.float32)
        rank = jnp.sum(hot * (counts + seen), axis=0, keepdims=True)
        seen = seen + jnp.sum(hot, axis=1, keepdims=True)
        at_rank = rank_of == rank
        high = lax.shift_right_logical(slot, 8)
        values = ((lane & 127) + 1, 2 * b + (lane >> 7), slot - high * 256, high)
        placed = jnp.concatenate(
            [jnp.where(at_rank, value.astype(jnp.float32), 0.0).astype(jnp.bfloat16) for value in values], axis=0)
        table = table + lax.dot_general(placed, hot16, (((1,), (1,)), ((), ())), preferred_element_type=jnp.float32)
    first, block, low, high = (
        jnp.concatenate([table[i * CAP : (i + 1) * CAP], jnp.zeros((LANES - CAP, OWNERS), jnp.float32)], axis=0).T.astype(jnp.int32) for i in range(4))
    filled = first > 0
    source_ref[...] = jnp.where(filled, block * LANES + first - 1, 0)
    key_ref[...] = jnp.where(filled, high * 256 + low, -1)

def tables(owner, slot, flag):
    shape = jax.ShapeDtypeStruct((OWNERS, LANES), jnp.int32)
    r = lambda v: v.reshape(16, 256)
    return pl.pallas_call(table_kernel, out_shape=(shape, shape), name="tables")(r(owner), r(slot), r(flag))


def fused_kernel(
    source_ref, key_ref, x_ref, out_ref,
    wide, picked, send, recv, keys_in, packed, up_in, down_in, acc,
    key_send, key_recv, row_send, row_recv, up_send, up_recv, down_send, down_recv,
):
    y, z, c, x = (lax.axis_index(name) for name in ALL)
    mine = y * 2 + c

    def peer(d):
        return ((y + d // 2 % 4) % 4, z, (c + d % 2) % 2, (x + d // 8) % 4)

    up, down = (y, (z + 1) % NZ, c, x), (y, (z + NZ - 1) % NZ, c, x)

    def copy_to(target, src, dst, send_sem, recv_sem):
        return pltpu.make_async_remote_copy(
            src_ref=src, dst_ref=dst, send_sem=send_sem, recv_sem=recv_sem,
            device_id=target, device_id_type=MESH,
        )

    barrier = pltpu.get_barrier_semaphore()

    def greet(d, _):
        pl.semaphore_signal(barrier, inc=1, device_id=peer(d), device_id_type=MESH)
        return 0

    lax.fori_loop(1, PLANE, greet, 0)
    for target in (up, down):
        pl.semaphore_signal(barrier, inc=1, device_id=target, device_id_type=MESH)

    def widen(i, _):
        part = x_ref[pl.ds(pl.multiple_of(i * 64, 64), 64), :]
        for f in range(4):
            wide[pl.ds(pl.multiple_of(i * 64, 64), 64), f, :] = part[:, f * LANES : (f + 1) * LANES].astype(
                jnp.float32
            )
        return 0

    lax.fori_loop(0, ROWS // 64, widen, 0)

    def gather(q):
        plane = (z + FAR_FIRST[q] + NZ) % NZ

        def pick(yc, _):
            base = pl.multiple_of(yc * CAP * 4, 4)
            for first in range(0, CAP, 16):
                got = [
                    wide[source_ref[yc * NZ + plane, first + k]]
                    for k in range(16)
                ]
                for k in range(16):
                    picked[pl.ds(base + (first + k) * 4, 4), :] = got[k]
            return 0

        lax.fori_loop(0, 8, pick, 0)

        def narrow(yc, _):
            for f in range(4):
                send[q, f, yc] = picked[pl.ds(yc * CAP * 4 + f, CAP, stride=4), :].astype(jnp.bfloat16)
            return 0

        lax.fori_loop(0, 8, narrow, 0)
        recv[q, 0:CAP, :] = send[q, x, mine]

    def start_rows(q):
        def go(d, _):
            target = peer(d)
            copy_to(
                target,
                send.at[q, target[3], target[0] * 2 + target[2]],
                recv.at[q, pl.ds(pl.multiple_of(d * CAP, CAP), CAP)],
                row_send.at[q], row_recv.at[q],
            ).start()
            return 0

        lax.fori_loop(1, PLANE, go, 0)

    def rows_of(q):
        rest = recv.at[q, pl.ds(CAP, (PLANE - 1) * CAP)]
        return copy_to(peer(1), rest, rest, row_send.at[q], row_recv.at[q])

    gather(0)
    pl.semaphore_wait(barrier, PLANE + 1)

    def send_keys(d, _):
        target = peer(d)
        copy_to(target, key_ref.at[target[0] * 2 + target[2]], keys_in.at[d], key_send, key_recv).start()
        return 0

    lax.fori_loop(1, PLANE, send_keys, 0)
    start_rows(0)
    keys_in[0] = key_ref[mine]
    gather(1)
    start_rows(1)
    gather(2)
    start_rows(2)

    all_keys = copy_to(peer(1), keys_in.at[pl.ds(1, PLANE - 1)], keys_in.at[pl.ds(1, PLANE - 1)], key_send, key_recv)
    all_keys.wait_recv()
    lane = lax.broadcasted_iota(jnp.int32, (NZ, LANES), 1)
    for m in range(PLANE // 4):
        k0, k1, k2, k3 = (keys_in[4 * m + i] for i in range(4))
        k1, k2, k3 = pltpu.roll(k1, 96, 1), pltpu.roll(k2, 64, 1), pltpu.roll(k3, 32, 1)
        packed[3 * m] = jnp.where(lane < 96, k0, k1)
        packed[3 * m + 1] = jnp.where(lane < 64, k1, k2)
        packed[3 * m + 2] = jnp.where(lane < 32, k2, k3)

    block = 768
    tiles = block // LANES
    slot_of = lax.broadcasted_iota(jnp.int32, (SLOTS, block), 0)

    def add_up(q):
        plane = (z + FAR_FIRST[q] + NZ) % NZ
        rows_of(q).wait_recv()

        def part(k):
            lanes = jnp.concatenate(
                [packed[k * tiles + i, pl.ds(plane, 1), :] for i in range(tiles)], axis=1
            )
            hot = jnp.where(slot_of == lanes, 1.0, 0.0).astype(jnp.bfloat16)
            rows = recv[q, pl.ds(pl.multiple_of(k * block, block), block), :]
            return jnp.dot(hot, rows, preferred_element_type=jnp.float32)

        acc[q] = part(0)

        def step(k, _):
            acc[q] += part(k)
            return 0

        lax.fori_loop(1, PLANE * CAP // block, step, 0)

    low, high, whole = pl.ds(0, HALF), pl.ds(HALF, HALF), pl.ds(0, SLOTS)

    def up_copy(q, r, part):
        return copy_to(up, acc.at[q, part], up_in.at[r - 1, part], up_send.at[r - 1], up_recv.at[r - 1])

    def down_copy(q, r, part):
        return copy_to(down, acc.at[q, part], down_in.at[r - 1, part], down_send.at[r - 1], down_recv.at[r - 1])

    for q, r in enumerate(FAR_FIRST):
        if q + 3 < len(FAR_FIRST):
            gather(q + 3)
            start_rows(q + 3)
        add_up(q)
        if r == 4:
            up_copy(q, 4, low).start()
            down_copy(q, 4, high).start()
        elif r > 0:
            part = low if r == 3 else whole
            up_copy(0, r + 1, part).wait_recv()
            acc[q, part, :] += up_in[r, part, :]
            up_copy(q, r, whole).start()
        elif r < 0:
            part = high if r == -3 else whole
            down_copy(0, 1 - r, part).wait_recv()
            acc[q, part, :] += down_in[-r, part, :]
            down_copy(q, -r, whole).start()
        else:
            up_copy(0, 1, whole).wait_recv()
            down_copy(0, 1, whole).wait_recv()
            out_ref[...] = acc[q] + up_in[0] + down_in[0]

    all_keys.wait_send()
    for q in range(len(FAR_FIRST)):
        rows_of(q).wait_send()
    for r in range(1, 5):
        up_copy(0, r, low if r == 4 else whole).wait_send()
        down_copy(0, r, high if r == 4 else whole).wait_send()


def light_totals(source, key, rows):
    vmem = pl.BlockSpec(memory_space=pltpu.VMEM)
    dma = pltpu.SemaphoreType.DMA
    return pl.pallas_call(
        fused_kernel,
        in_specs=[pl.BlockSpec(memory_space=pltpu.SMEM), vmem, vmem],
        out_specs=vmem,
        out_shape=jax.ShapeDtypeStruct((SLOTS, LANES), jnp.float32),
        scratch_shapes=[
            pltpu.VMEM((ROWS, 4, LANES), jnp.float32),
            pltpu.VMEM((8 * CAP * 4, LANES), jnp.float32),
            pltpu.VMEM((NZ, NX, 8, CAP, LANES), jnp.bfloat16),
            pltpu.VMEM((NZ, PLANE * CAP, LANES), jnp.bfloat16),
            pltpu.VMEM((PLANE, NZ, LANES), jnp.int32),
            pltpu.VMEM((PLANE * CAP // LANES, NZ, LANES), jnp.int32),
            pltpu.VMEM((4, SLOTS, LANES), jnp.float32),
            pltpu.VMEM((4, SLOTS, LANES), jnp.float32),
            pltpu.VMEM((NZ, SLOTS, LANES), jnp.float32),
            dma, dma, dma((NZ,)), dma((NZ,)), dma((4,)), dma((4,)), dma((4,)), dma((4,)),
        ],
        compiler_params=pltpu.CompilerParams(
            collective_id=0, has_side_effects=True, vmem_limit_bytes=62 << 20
        ),
        name="light_totals",
    )(source, key.reshape(8, NZ, LANES), rows)


def split_up(value, dim, count):
    dims = value.shape
    pieces = value.reshape(*dims[:dim], count, dims[dim] // count, *dims[dim + 1 :])
    return jnp.moveaxis(pieces, dim, 0)


def sum_at_owner(value, axis, dim):
    count = lax.axis_size(axis)
    pieces = lax.all_to_all(split_up(value, dim, count), axis, 0, 0, tiled=True)
    return jnp.sum(pieces, axis=0)


def summed_rows(value, axes, dim):
    far, near = axes
    pieces = split_up(value, dim, lax.axis_size(far))
    nearer = sum_at_owner(pieces, near, dim + 1)
    arrived = lax.all_to_all(nearer, far, split_axis=0, concat_axis=0, tiled=True)
    return arrived.sum(axis=0)


def heavy_kernel(key_ref, x_ref, out_ref):
    slot_of = lax.broadcasted_iota(jnp.int32, (H, 512), 0)
    lanes = jnp.concatenate([key_ref[0, i : i + 1, :] for i in range(4)], axis=1)
    hot = jnp.where(slot_of == lanes, 1.0, 0.0).astype(jnp.bfloat16)
    part = jnp.dot(hot, x_ref[...], preferred_element_type=jnp.float32)

    @pl.when(pl.program_id(0) == 0)
    def _():
        out_ref[...] = part

    @pl.when(pl.program_id(0) > 0)
    def _():
        out_ref[...] += part


def heavy_partial(key, rows):
    return pl.pallas_call(
        heavy_kernel,
        grid=(8,),
        in_specs=[
            pl.BlockSpec((1, 4, LANES), lambda i: (i, 0, 0)),
            pl.BlockSpec((512, F), lambda i: (i, 0)),
        ],
        out_specs=pl.BlockSpec((H, F), lambda i: (0, 0)),
        out_shape=jax.ShapeDtypeStruct((H, F), jnp.float32),
        name="heavy_partial",
    )(key.reshape(8, 4, LANES), rows)


def shards(rows, owner, slot, flag, heavy_key, light_dims, heavy_dims):
    owner, slot, flag, heavy_key = (v.reshape(ROWS) for v in (owner, slot, flag, heavy_key))
    source, key = tables(owner, slot, flag)
    totals = light_totals(source, key, rows)
    light_joined = (totals * light_dims.astype(jnp.float32)).astype(jnp.bfloat16)
    heavy = heavy_partial(jnp.where(flag == 1, heavy_key, -1), rows)
    shares = summed_rows(heavy, (("y", "z"), ("c", "x")), 0)
    joined_here = (shares * heavy_dims.astype(jnp.float32)).astype(jnp.bfloat16)
    heavy_joined = lax.all_gather(joined_here, ALL, axis=0, tiled=True)
    return light_joined, heavy_joined


def solution(mesh):
    torus = Mesh(mesh.devices.reshape(NY, NZ, NC, NX), ALL)
    rows = P(ALL, None)
    return jax.shard_map(
        shards,
        mesh=torus,
        in_specs=(rows, rows, rows, rows, rows, P(SHUFFLE, "x"), rows),
        out_specs=(P(SHUFFLE, "x"), P()),
        check_vma=False,
    )
```

time: 378 us -> 194 us (0.51)
  waiting for transfers between devices: 175 us -> 3.88 us
  Pallas kernels: 0 us -> 110 us
  blocking collectives: 0 us -> 52.5 us
  local copies, waits for them, and re-layouts: 58.9 us -> 6.77 us
  matrix products: 45.2 us -> 0 us
  other arithmetic: 43.5 us -> 6.25 us
  starting transfers between devices: 36.9 us -> 0.04 us
    all_to_all x5 -> x0, waiting for transfers between devices: 175 us -> none  [the longest x1 143 us: shards(): lax.all_to_all(buffer, SHUFFLE, split_axis=0, concat_axis=0, tiled=True)]
    pallas_call x0 -> x3, Pallas kernels: none -> 110 us  [the longest x1 95.4 us: light_totals(): pl.pallas_call(fused_kernel, in_specs=[pl.BlockSpec(memory_space=pltpu.SM...]
    all_to_all x0 -> x2, blocking collectives: none -> 52.5 us  [the longest x1 31.8 us: sum_at_owner(): pieces = lax.all_to_all(split_up(value, dim, count), axis, 0, 0, tiled=True)]
    dot_general x8 -> x0, matrix products: 45.2 us -> none  [pick_block(): lax.dot_general(onehot, values, (((0,), (0,)), ((), ())), preferred_eleme...]
    scatter x2 -> x0, local copies, waits for them, and re-layouts: 38 us -> none  [the longest x1 22.4 us: bucket(): buffer = jnp.zeros((groups * capacity, values.shape[1]), values.dtype).at...]
    all_to_all x5 -> x0, starting transfers between devices: 36.9 us -> none  [the longest x2 11.3 us: sum_at_owner(): pieces = lax.all_to_all(split_up(value, dim, count), axis, 0, 0, tiled=True)]
    another operation x2 -> x0, other arithmetic: 32.5 us -> none
    transpose x2 -> x0, local copies, waits for them, and re-layouts: 6.43 us -> none  [split_up(): return jnp.moveaxis(pieces, dim, 0)]
  transfers between devices with their start and end apart: 6 -> 1, of which waited for: 3 -> 1; matrix products, arithmetic and copies ran while one was open for 32% -> 3% of each run, Pallas kernels for 0% -> 52%
where the time goes in v2:
time: 194 us; the launch traced here: 193 us
  Pallas kernels  110 us (57%)
  blocking collectives  52.5 us (27%)
  between operations  14.1 us (7%)
  local copies, waits for them, and re-layouts  6.77 us (3%)
  other arithmetic  6.25 us (3%)
  waiting for transfers between devices  3.88 us (2%)
    pallas_call x1, Pallas kernels, light_totals(): pl.pallas_call(fused_kernel, in_specs=[pl.BlockSpec(memory_space=pltpu.SM...  95.4 us
    all_to_all x1, blocking collectives, sum_at_owner(): pieces = lax.all_to_all(split_up(value, dim, count), axis, 0, 0, tiled=True)  31.8 us
    all_to_all x1, blocking collectives, summed_rows(): lax.all_to_all(nearer, far, split_axis=0, concat_axis=0, tiled=True)  20.6 us
    pallas_call x1, Pallas kernels, heavy_partial(): pl.pallas_call(heavy_kernel, grid=(8,), in_specs=[pl.BlockSpec((1, 4, LAN...  10.1 us
    pallas_call x1, Pallas kernels, tables(): pl.pallas_call(table_kernel, out_shape=(shape, shape), name='tables')  4.17 us
  transfers between devices with their start and end apart: 1, of which 1 were waited for; matrix products, arithmetic and copies ran while one was open for 3% of the time, Pallas kernels for 52%

profile of v2, /device:TPU:1, one launch (start us, length us, event | category | flops | bytes accessed | tf_op | source)
XLA Modules:
  0.0 193.2 jit_solution(1842597536926361600)
XLA Ops:
  7.2 0.0 all-gather.3.cloned.1.call-start
  7.2 0.5 broadcast.15
  7.7 2.0 %compare_select_fusion = (s32[4096,1]{0,1:T(1,128)}, s32[4096]{0:T(1024)S(1)}) fusion(s32[4096,1]{0,1:T(1,128)} %param.11, s32[4096,1]{0,1:T(1,128)} %param.10, s32[]{:T(128)} %broadcast.15), kind=kLoop, calls=%fused_computation.2 | loop fusion | flops 8192 | bytes 65540 | tf_op jit(solution)/shard_map/jit(_where)/select_n | solution.py:316
  9.7 10.1 %heavy_partial.1 = f32[1024,512]{1,0:T(8,128)} custom-call(s32[8,4,128]{2,1,0:T(4,128)} %bitcast.11, bf16[4096,512]{1,0:T(8,128)(2,1)} %x_ref.3), custom_call_target="tpu_custom_call" | custom-call | tf_op jit(solution)/shard_map/heavy_partial/pallas_call | solution.py:298
  19.8 1.9 reshape_reshape.15
  21.7 0.4 copy.15
  22.1 31.8 %all_to_all.10 = f32[8,32,4,512]{3,2,1,0:T(4,128)S(1)} all-to-all(f32[8,32,4,512]{3,2,1,0:T(4,128)S(1)} %bitcast.10), channel_id=1, replica_groups=mesh['y'=4,'z'=8,'c'=2,'x'=4] {'c','x'}, dimensions={0} | all-to-all | bytes 4194304 | tf_op jit(solution)/shard_map/all_to_all | solution.py:270
  53.9 0.0 copy-start.3
  53.9 0.0 copy-start.1
  53.9 0.0 copy-start.2
  53.9 0.4 reduce_sum.18
  54.4 20.6 %all_to_all.11 = f32[32,4,512]{2,1,0:T(4,128)S(1)} all-to-all(f32[32,4,512]{2,1,0:T(4,128)S(1)} %reduce_sum.18), channel_id=1, replica_groups=mesh['y'=4,'z'=8,'c'=2,'x'=4] {'y','z'}, dimensions={0} | all-to-all | bytes 524288 | tf_op jit(solution)/shard_map/all_to_all | solution.py:278
  75.0 0.1 reduce_sum.19
  75.1 0.0 copy-done.3
  75.1 0.6 fusion
  75.7 0.0 all-gather.3.cloned.1.call-update
  75.7 0.0 copy-done.1
  75.7 0.7 reduce.9
  76.4 0.6 reshape_reshape.12.owner_ref
  77.0 0.0 copy-done.2
  77.0 0.7 reduce.10
  77.7 0.6 reshape_reshape.13.slot_ref
  78.3 0.6 reshape_reshape.14.flag_ref
  78.9 4.2 %tables.1 = (s32[64,128]{1,0:T(8,128)}, s32[64,128]{1,0:T(8,128)}) custom-call(s32[16,256]{1,0:T(8,128)} %reshape_reshape.12.owner_ref, s32[16,256]{1,0:T(8,128)} %reshape_reshape.13.slot_ref, s32[16,256]{1,0:T(8,128)} %reshape_reshape.14.flag_ref), custom_call_target="tpu_custom_call" | custom-call | tf_op jit(solution)/shard_map/tables/pallas_call | solution.py:63
  83.1 0.0 copy-start
  83.1 95.4 %light_totals.1 = f32[1024,128]{1,0:T(8,128)} custom-call(s32[64,128]{1,0:T(8,128)} %get-tuple-element.4.source_ref, s32[8,8,128]{2,1,0:T(8,128)} %bitcast.12, bf16[4096,512]{1,0:T(8,128)(2,1)} %x_ref.3), custom_call_target="tpu_custom_call" | custom-call | tf_op jit(solution)/shard_map/light_totals/pallas_call | solution.py:238
  178.5 0.0 copy-done
  178.5 1.8 multiply_convert_fusion
  180.3 3.9 %all-gather.3.cloned.1.call-done = bf16[256,4,512]{2,1,0:T(4,128)(2,1)} async-done(((bf16[1,4,512]{2,1,0:T(4,128)(2,1)}), bf16[256,4,512]{2,1,0:T(4,128)(2,1)}) %all-gather.3.cloned.1.call-update) | async-done | bytes 1048592 | tf_op jit(solution)/shard_map/all_gather | solution.py:319
  184.2 2.1 %reshape.18 = bf16[1024,512]{1,0:T(8,128)(2,1)} reshape(bf16[256,4,512]{2,1,0:T(4,128)(2,1)} %all-gather.3.cloned.1.call-done) | data formatting | bytes 2097152
Async XLA Ops:
  7.2 177.0 %all-gather.3.cloned.1.call-start = ((), (), s32[]{:S(2)}) async-start(), calls=%async_computation.2 | async-start | bytes 1052672 | tf_op jit(solution)/shard_map/all_gather | solution.py:319
  53.9 21.1 %copy-start.3 = (bf16[4,512]{1,0:T(4,128)(2,1)S(1)}, bf16[4,512]{1,0:T(4,128)(2,1)}, u32[]{:S(2)}) copy-start(bf16[4,512]{1,0:T(4,128)(2,1)} %param.13) | copy-start | bytes 12292
  53.9 21.7 %copy-start.1 = (s32[4096,1]{0,1:T(1,128)S(1)}, s32[4096,1]{0,1:T(1,128)}, u32[]{:S(2)}) copy-start(s32[4096,1]{0,1:T(1,128)} %param.8) | copy-start | bytes 49156
  53.9 23.0 %copy-start.2 = (s32[4096,1]{0,1:T(1,128)S(1)}, s32[4096,1]{0,1:T(1,128)}, u32[]{:S(2)}) copy-start(s32[4096,1]{0,1:T(1,128)} %param.9) | copy-start | bytes 49156
  83.1 95.4 %copy-start = (bf16[1024,128]{1,0:T(8,128)(2,1)S(1)}, bf16[1024,128]{1,0:T(8,128)(2,1)}, u32[]{:S(2)}) copy-start(bf16[1024,128]{1,0:T(8,128)(2,1)} %param.12) | copy-start | bytes 786436
Sparse Core Ops, SparseCore 0:
  75.8 108.3 all-gather.2

commit v3 on v2

--- a/solution.py
+++ b/solution.py
@@ -36,10 +36,12 @@
     seen = jnp.zeros((OWNERS, 1), jnp.float32)
     table = jnp.zeros((4 * CAP, OWNERS), jnp.float32)
     for b in range(ROWS // K):
-        owner = owner_ref[b : b + 1, :]
+        owner, slot, flag = (
+            jnp.concatenate([ref[2 * b : 2 * b + 1, :], ref[2 * b + 1 : 2 * b + 2, :]], axis=1)
+            for ref in (owner_ref, slot_ref, flag_ref)
+        )
         owner = (owner >> 4) * 16 + (owner & 1) * 8 + ((owner >> 1) & 7)
-        owner = jnp.where(flag_ref[b : b + 1, :] == 0, owner, -1)
-        slot = slot_ref[b : b + 1, :]
+        owner = jnp.where(flag == 0, owner, -1)
         hot = jnp.where(owner_of == owner, 1.0, 0.0)
         hot16 = hot.astype(jnp.bfloat16)
         counts = jnp.dot(hot16, before, preferred_element_type=jnp.float32)
@@ -59,14 +61,16 @@
 
 def tables(owner, slot, flag):
     shape = jax.ShapeDtypeStruct((OWNERS, LANES), jnp.int32)
-    r = lambda v: v.reshape(16, 256)
-    return pl.pallas_call(table_kernel, out_shape=(shape, shape), name="tables")(r(owner), r(slot), r(flag))
+    return pl.pallas_call(table_kernel, out_shape=(shape, shape), name="tables")(owner, slot, flag)
 
 
 def fused_kernel(
-    source_ref, key_ref, x_ref, out_ref,
+    source_ref, key_ref, hkey_ref, flag_ref, x_ref, dims_ref, hdims_ref, out_ref, hout,
     wide, picked, send, recv, keys_in, packed, up_in, down_in, acc,
+    hacc, half_in, hrun, hup_in, hdown_in, hpart, plane_in,
     key_send, key_recv, row_send, row_recv, up_send, up_recv, down_send, down_recv,
+    half_send, half_recv, hup_send, hup_recv, hdown_send, hdown_recv, part_send, part_recv,
+    line_send, line_recv, sheet_send, sheet_recv, twin_send, twin_recv,
 ):
     y, z, c, x = (lax.axis_index(name) for name in ALL)
     mine = y * 2 + c
@@ -89,8 +93,20 @@
         return 0
 
     lax.fori_loop(1, PLANE, greet, 0)
-    for target in (up, down):
-        pl.semaphore_signal(barrier, inc=1, device_id=target, device_id_type=MESH)
+
+    def along(d):
+        return (y, (z + d) % NZ, c, x)
+
+    def across(d):
+        return ((y + d % 4) % 4, z, c, (x + d // 4) % 4)
+
+    twin = (y, z, 1 - c, x)
+
+    def greet_line(d, _):
+        pl.semaphore_signal(barrier, inc=1, device_id=along(d), device_id_type=MESH)
+        return 0
+
+    lax.fori_loop(1, NZ, greet_line, 0)
 
     def widen(i, _):
         part = x_ref[pl.ds(pl.multiple_of(i * 64, 64), 64), :]
@@ -144,7 +160,7 @@
         return copy_to(peer(1), rest, rest, row_send.at[q], row_recv.at[q])
 
     gather(0)
-    pl.semaphore_wait(barrier, PLANE + 1)
+    pl.semaphore_wait(barrier, PLANE + NZ - 2)
 
     def send_keys(d, _):
         target = peer(d)
@@ -156,8 +172,31 @@
     keys_in[0] = key_ref[mine]
     gather(1)
     start_rows(1)
-    gather(2)
-    start_rows(2)
+
+    heavy_of = lax.broadcasted_iota(jnp.int32, (H, F), 0)
+
+    def heavy_block(b):
+        lanes = []
+        for i in range(4):
+            k = hkey_ref[pl.ds(b * 4 + i, 1), :]
+            k = ((k >> 4) & 1) * 512 + ((k >> 5) & 7) * 64 + (k >> 8) * 16 + (k & 15)
+            lanes.append(jnp.where(flag_ref[pl.ds(b * 4 + i, 1), :] == 1, k, -1))
+        hot = jnp.where(heavy_of == jnp.concatenate(lanes, axis=1), 1.0, 0.0).astype(jnp.bfloat16)
+        rows = x_ref[pl.ds(pl.multiple_of(b * 512, 512), 512), :]
+        return jnp.dot(hot, rows, preferred_element_type=jnp.float32)
+
+    hacc[...] = heavy_block(0)
+
+    def heavy_step(b, _):
+        hacc[...] += heavy_block(b)
+        return 0
+
+    lax.fori_loop(1, ROWS // 512, heavy_step, 0)
+    halves = H // 2
+    half_copy = copy_to(
+        twin, hacc.at[pl.ds(pl.multiple_of((1 - c) * halves, halves), halves)], half_in, half_send, half_recv
+    )
+    half_copy.start()
 
     all_keys = copy_to(peer(1), keys_in.at[pl.ds(1, PLANE - 1)], keys_in.at[pl.ds(1, PLANE - 1)], key_send, key_recv)
     all_keys.wait_recv()
@@ -201,10 +240,111 @@
     def down_copy(q, r, part):
         return copy_to(down, acc.at[q, part], down_in.at[r - 1, part], down_send.at[r - 1], down_recv.at[r - 1])
 
+    hlow, hhigh, hwhole = pl.ds(0, 32), pl.ds(32, 32), pl.ds(0, 64)
+
+    def hup_copy(r, part):
+        return copy_to(
+            up, hrun.at[(z + r) % NZ, part], hup_in.at[r - 1, part], hup_send.at[r - 1], hup_recv.at[r - 1]
+        )
+
+    def hdown_copy(r, part):
+        return copy_to(
+            down, hrun.at[(z + NZ - r) % NZ, part], hdown_in.at[r - 1, part],
+            hdown_send.at[r - 1], hdown_recv.at[r - 1],
+        )
+
+    def heavy_far():
+        half_copy.wait_recv()
+
+        def own(i, _):
+            rows = pl.ds(pl.multiple_of(i * 64, 64), 64)
+            hrun[i] = hacc[pl.ds(pl.multiple_of(c * halves + i * 64, 64), 64), :] + half_in[rows, :]
+            return 0
+
+        lax.fori_loop(0, NZ, own, 0)
+        hup_copy(4, hlow).start()
+        hdown_copy(4, hhigh).start()
+
+    def heavy_on(r):
+        part = hlow if r == 3 else hwhole
+        hup_copy(r + 1, part).wait_recv()
+        hrun[(z + r) % NZ, part, :] += hup_in[r, part, :]
+        hup_copy(r, hwhole).start()
+        part = hhigh if r == 3 else hwhole
+        hdown_copy(r + 1, part).wait_recv()
+        hrun[(z + NZ - r) % NZ, part, :] += hdown_in[r, part, :]
+        hdown_copy(r, hwhole).start()
+
+    def part_copy(d):
+        target = across(d)
+        return copy_to(
+            target, hpart.at[target[0] * 4 + target[3]], plane_in.at[d], part_send.at[d], part_recv.at[d]
+        )
+
+    def heavy_plane():
+        hup_copy(1, hwhole).wait_recv()
+        hdown_copy(1, hwhole).wait_recv()
+        hrun[z] += hup_in[0] + hdown_in[0]
+        for i in range(16):
+            hpart[i] = hrun[z, pl.ds(4 * i, 4), :]
+        lax.fori_loop(1, 16, lambda d, _: (part_copy(d).start(), 0)[1], 0)
+
+    def line_copy(d):
+        return copy_to(
+            along(d), hout.at[y, z, c, x], hout.at[y, z, c, x], line_send.at[d], line_recv.at[d]
+        )
+
+    def line_from(d):
+        spot = hout.at[y, (z + NZ - d) % NZ, c, x]
+        return copy_to(along(d), spot, spot, line_send.at[d], line_recv.at[d])
+
+    def heavy_join():
+        lax.fori_loop(1, 16, lambda d, _: (part_copy(d).wait_recv(), 0)[1], 0)
+        total = hpart[y * 4 + x]
+        for d in range(1, 16):
+            total += plane_in[d]
+        hout[y, z, c, x] = (total * hdims_ref[...].astype(jnp.float32)).astype(jnp.bfloat16)
+        lax.fori_loop(1, NZ, lambda d, _: (line_copy(d).start(), 0)[1], 0)
+
+    def sheet_copy(d):
+        spot = hout.at[y, :, c, x]
+        return copy_to(across(d), spot, spot, sheet_send.at[d], sheet_recv.at[d])
+
+    def sheet_from(d):
+        spot = hout.at[(y + 4 - d % 4) % 4, :, c, (x + 4 - d // 4) % 4]
+        return copy_to(across(d), spot, spot, sheet_send.at[d], sheet_recv.at[d])
+
+    def heavy_sheet():
+        lax.fori_loop(1, NZ, lambda d, _: (line_from(d).wait_recv(), 0)[1], 0)
+        lax.fori_loop(1, 16, lambda d, _: (sheet_copy(d).start(), 0)[1], 0)
+
+    def twin_copy(core):
+        spot = hout.at[:, :, core]
+        return copy_to(twin, spot, spot, twin_send, twin_recv)
+
+    def heavy_twin():
+        lax.fori_loop(1, 16, lambda d, _: (sheet_from(d).wait_recv(), 0)[1], 0)
+        twin_copy(c).start()
+
+    ahead = {
+        0: heavy_far,
+        1: lambda: heavy_on(2),
+        2: heavy_plane,
+        5: heavy_join,
+    }
+    behind = {
+        0: lambda: heavy_on(3),
+        1: lambda: heavy_on(1),
+        6: heavy_sheet,
+        7: heavy_twin,
+    }
+
     for q, r in enumerate(FAR_FIRST):
-        if q + 3 < len(FAR_FIRST):
-            gather(q + 3)
-            start_rows(q + 3)
+        if q in ahead:
+            ahead[q]()
+        if q + 2 < len(FAR_FIRST):
+            gather(q + 2)
+            start_rows(q + 2)
         add_up(q)
         if r == 4:
             up_copy(q, 4, low).start()
@@ -222,102 +362,74 @@
         else:
             up_copy(0, 1, whole).wait_recv()
             down_copy(0, 1, whole).wait_recv()
-            out_ref[...] = acc[q] + up_in[0] + down_in[0]
-
+            total = acc[q] + up_in[0] + down_in[0]
+            out_ref[...] = (total * dims_ref[...].astype(jnp.float32)).astype(jnp.bfloat16)
+        if q in behind:
+            behind[q]()
+
+    twin_copy(1 - c).wait_recv()
+    twin_copy(c).wait_send()
+    half_copy.wait_send()
+    lax.fori_loop(1, 16, lambda d, _: (part_copy(d).wait_send(), 0)[1], 0)
+    lax.fori_loop(1, 16, lambda d, _: (sheet_copy(d).wait_send(), 0)[1], 0)
+    lax.fori_loop(1, NZ, lambda d, _: (line_copy(d).wait_send(), 0)[1], 0)
     all_keys.wait_send()
     for q in range(len(FAR_FIRST)):
         rows_of(q).wait_send()
     for r in range(1, 5):
         up_copy(0, r, low if r == 4 else whole).wait_send()
         down_copy(0, r, high if r == 4 else whole).wait_send()
-
-
-def light_totals(source, key, rows):
+        hup_copy(r, hlow if r == 4 else hwhole).wait_send()
+        hdown_copy(r, hhigh if r == 4 else hwhole).wait_send()
+
+
+def join(source, key, heavy_key, flag, rows, light_dims, heavy_dims):
     vmem = pl.BlockSpec(memory_space=pltpu.VMEM)
     dma = pltpu.SemaphoreType.DMA
+    f32 = jnp.float32
     return pl.pallas_call(
         fused_kernel,
-        in_specs=[pl.BlockSpec(memory_space=pltpu.SMEM), vmem, vmem],
-        out_specs=vmem,
-        out_shape=jax.ShapeDtypeStruct((SLOTS, LANES), jnp.float32),
+        in_specs=[pl.BlockSpec(memory_space=pltpu.SMEM)] + [vmem] * 6,
+        out_specs=(vmem, vmem),
+        out_shape=(
+            jax.ShapeDtypeStruct((SLOTS, LANES), jnp.bfloat16),
+            jax.ShapeDtypeStruct((NY, NZ, NC, NX, 4, F), jnp.bfloat16),
+        ),
         scratch_shapes=[
-            pltpu.VMEM((ROWS, 4, LANES), jnp.float32),
-            pltpu.VMEM((8 * CAP * 4, LANES), jnp.float32),
+            pltpu.VMEM((ROWS, 4, LANES), f32),
+            pltpu.VMEM((8 * CAP * 4, LANES), f32),
             pltpu.VMEM((NZ, NX, 8, CAP, LANES), jnp.bfloat16),
             pltpu.VMEM((NZ, PLANE * CAP, LANES), jnp.bfloat16),
             pltpu.VMEM((PLANE, NZ, LANES), jnp.int32),
             pltpu.VMEM((PLANE * CAP // LANES, NZ, LANES), jnp.int32),
-            pltpu.VMEM((4, SLOTS, LANES), jnp.float32),
-            pltpu.VMEM((4, SLOTS, LANES), jnp.float32),
-            pltpu.VMEM((NZ, SLOTS, LANES), jnp.float32),
+            pltpu.VMEM((4, SLOTS, LANES), f32),
+            pltpu.VMEM((4, SLOTS, LANES), f32),
+            pltpu.VMEM((NZ, SLOTS, LANES), f32),
+            pltpu.VMEM((H, F), f32),
+            pltpu.VMEM((H // 2, F), f32),
+            pltpu.VMEM((NZ, 64, F), f32),
+            pltpu.VMEM((4, 64, F), f32),
+            pltpu.VMEM((4, 64, F), f32),
+            pltpu.VMEM((16, 4, F), f32),
+            pltpu.VMEM((16, 4, F), f32),
             dma, dma, dma((NZ,)), dma((NZ,)), dma((4,)), dma((4,)), dma((4,)), dma((4,)),
+            dma, dma, dma((4,)), dma((4,)), dma((4,)), dma((4,)), dma((16,)), dma((16,)),
+            dma((NZ,)), dma((NZ,)), dma((16,)), dma((16,)), dma, dma,
         ],
         compiler_params=pltpu.CompilerParams(
             collective_id=0, has_side_effects=True, vmem_limit_bytes=62 << 20
         ),
-        name="light_totals",
-    )(source, key.reshape(8, NZ, LANES), rows)
-
-
-def split_up(value, dim, count):
-    dims = value.shape
-    pieces = value.reshape(*dims[:dim], count, dims[dim] // count, *dims[dim + 1 :])
-    return jnp.moveaxis(pieces, dim, 0)
-
-
-def sum_at_owner(value, axis, dim):
-    count = lax.axis_size(axis)
-    pieces = lax.all_to_all(split_up(value, dim, count), axis, 0, 0, tiled=True)
-    return jnp.sum(pieces, axis=0)
-
-
-def summed_rows(value, axes, dim):
-    far, near = axes
-    pieces = split_up(value, dim, lax.axis_size(far))
-    nearer = sum_at_owner(pieces, near, dim + 1)
-    arrived = lax.all_to_all(nearer, far, split_axis=0, concat_axis=0, tiled=True)
-    return arrived.sum(axis=0)
-
-
-def heavy_kernel(key_ref, x_ref, out_ref):
-    slot_of = lax.broadcasted_iota(jnp.int32, (H, 512), 0)
-    lanes = jnp.concatenate([key_ref[0, i : i + 1, :] for i in range(4)], axis=1)
-    hot = jnp.where(slot_of == lanes, 1.0, 0.0).astype(jnp.bfloat16)
-    part = jnp.dot(hot, x_ref[...], preferred_element_type=jnp.float32)
-
-    @pl.when(pl.program_id(0) == 0)
-    def _():
-        out_ref[...] = part
-
-    @pl.when(pl.program_id(0) > 0)
-    def _():
-        out_ref[...] += part
-
-
-def heavy_partial(key, rows):
-    return pl.pallas_call(
-        heavy_kernel,
-        grid=(8,),
-        in_specs=[
-            pl.BlockSpec((1, 4, LANES), lambda i: (i, 0, 0)),
-            pl.BlockSpec((512, F), lambda i: (i, 0)),
-        ],
-        out_specs=pl.BlockSpec((H, F), lambda i: (0, 0)),
-        out_shape=jax.ShapeDtypeStruct((H, F), jnp.float32),
-        name="heavy_partial",
-    )(key.reshape(8, 4, LANES), rows)
+        name="join",
+    )(source, key.reshape(8, NZ, LANES), heavy_key, flag, rows, light_dims, heavy_dims)
 
 
 def shards(rows, owner, slot, flag, heavy_key, light_dims, heavy_dims):
-    owner, slot, flag, heavy_key = (v.reshape(ROWS) for v in (owner, slot, flag, heavy_key))
+    owner, slot, flag, heavy_key = (
+        v.reshape(ROWS // LANES, LANES) for v in (owner, slot, flag, heavy_key)
+    )
     source, key = tables(owner, slot, flag)
-    totals = light_totals(source, key, rows)
-    light_joined = (totals * light_dims.astype(jnp.float32)).astype(jnp.bfloat16)
-    heavy = heavy_partial(jnp.where(flag == 1, heavy_key, -1), rows)
-    shares = summed_rows(heavy, (("y", "z"), ("c", "x")), 0)
-    joined_here = (shares * heavy_dims.astype(jnp.float32)).astype(jnp.bfloat16)
-    heavy_joined = lax.all_gather(joined_here, ALL, axis=0, tiled=True)
-    return light_joined, heavy_joined
+    light_joined, heavy_joined = join(source, key, heavy_key, flag, rows, light_dims, heavy_dims)
+    return light_joined, heavy_joined.reshape(H, F)
 
 
 def solution(mesh):

time: 194 us -> 124 us (0.64)
  blocking collectives: 52.5 us -> 0 us
  between operations: 14.1 us -> 0.64 us
  Pallas kernels: 110 us -> 120 us
  other arithmetic: 6.25 us -> 0 us
  waiting for transfers between devices: 3.88 us -> 0 us
  local copies, waits for them, and re-layouts: 6.77 us -> 3.81 us
    all_to_all x2 -> x0, blocking collectives: 52.5 us -> none  [the longest x1 31.8 us: sum_at_owner(): pieces = lax.all_to_all(split_up(value, dim, count), axis, 0, 0, tiled=True)]
    pallas_call x2 -> x1, Pallas kernels: 105 us -> 116 us  [join(): pl.pallas_call(fused_kernel, in_specs=[pl.BlockSpec(memory_space=pltpu.SM...]
    another operation x5 -> x0, local copies, waits for them, and re-layouts: 4.11 us -> none  [the longest x2 2.3 us: split_up(): value.reshape(*dims[:dim], count, dims[dim] // count, *dims[dim + 1:])]
    all_gather x1 -> x0, waiting for transfers between devices: 3.86 us -> none  [shards(): heavy_joined = lax.all_gather(joined_here, ALL, axis=0, tiled=True)]
    reshape x0 -> x1, local copies, waits for them, and re-layouts: none -> 2.14 us  [shards(): return (light_joined, heavy_joined.reshape(H, F))]
    select_n x1 -> x0, other arithmetic: 2.01 us -> none  [shards(): heavy = heavy_partial(jnp.where(flag == 1, heavy_key, -1), rows)]
    unnamed x3 -> x0, other arithmetic: 1.97 us -> none
  transfers between devices with their start and end apart: 1 -> 0, of which waited for: 1 -> 0; matrix products, arithmetic and copies ran while one was open for 3% -> 0% of each run, Pallas kernels for 52% -> 0%
where the time goes in v3:
time: 124 us
  Pallas kernels  120 us (97%)
  local copies, waits for them, and re-layouts  3.81 us (3%)
    pallas_call x1, Pallas kernels, join(): pl.pallas_call(fused_kernel, in_specs=[pl.BlockSpec(memory_space=pltpu.SM...  116 us
    pallas_call x1, Pallas kernels, tables(): pl.pallas_call(table_kernel, out_shape=(shape, shape), name='tables')  4.18 us

profile of v3, /device:TPU:1, one launch (start us, length us, event | category | flops | bytes accessed | tf_op | source)
XLA Modules:
  0.0 124.3 jit_solution(9026120890728597913)
XLA Ops:
  0.6 4.2 %tables.1 = (s32[64,128]{1,0:T(8,128)}, s32[64,128]{1,0:T(8,128)}) custom-call(s32[32,128]{1,0:T(8,128)} %bitcast.9, s32[32,128]{1,0:T(8,128)} %bitcast.10, s32[32,128]{1,0:T(8,128)} %bitcast.5), custom_call_target="tpu_custom_call" | custom-call | tf_op jit(solution)/shard_map/tables/pallas_call | solution.py:64
  4.8 115.6 %join.1 = (bf16[1024,128]{1,0:T(8,128)(2,1)}, bf16[4,8,2,4,4,512]{5,4,3,2,1,0:T(4,128)(2,1)}) custom-call(s32[64,128]{1,0:T(8,128)} %get-tuple-element.6.source_ref, s32[8,8,128]{2,1,0:T(8,128)} %bitcast.7, s32[32,128]{1,0:T(8,128)} %bitcast.8, s32[32,128]{1,0:T(8,128)} %bitcast.6, bf16[4096,512]{1,0:T(8,128)(2,1)} %x_ref.1, bf16[1024,128]{1,0:T(8,128)(2,1)} %dims_ref.1, ...), custom_call_target="tpu_custom_call" | custom-call | tf_op jit(solution)/shard_map/join/pallas_call | solution.py:390
  120.4 2.1 %reshape.27 = bf16[1024,512]{1,0:T(8,128)(2,1)} reshape(bf16[4,8,2,4,4,512]{5,4,3,2,1,0:T(4,128)(2,1)} %get-tuple-element.9) | data formatting | bytes 2097152 | tf_op jit(solution)/shard_map/reshape | solution.py:432
  122.6 1.7 %copy.10 = bf16[1024,128]{1,0:T(8,128)(2,1)} copy(bf16[1024,128]{1,0:T(8,128)(2,1)} %get-tuple-element.12) | data formatting | bytes 524288

commit v4 on v3

--- a/solution.py
+++ b/solution.py
@@ -22,6 +22,7 @@
 MESH = pl.DeviceIdType.MESH
 FAR_FIRST = (4, 3, -3, 2, -2, 1, -1, 0)
 HALF = SLOTS // 2
+X_PART = 256
 
 
 def table_kernel(owner_ref, slot_ref, flag_ref, source_ref, key_ref):
@@ -65,8 +66,8 @@
 
 
 def fused_kernel(
-    source_ref, key_ref, hkey_ref, flag_ref, x_ref, dims_ref, hdims_ref, out_ref, hout,
-    wide, picked, send, recv, keys_in, packed, up_in, down_in, acc,
+    source_ref, key_ref, hkey_ref, flag_ref, x_hbm, dims_ref, hdims_ref, out_ref, hout,
+    x_ref, x_sem, wide, picked, send, recv, keys_in, packed, up_in, down_in, acc,
     hacc, half_in, hrun, hup_in, hdown_in, hpart, plane_in,
     key_send, key_recv, row_send, row_recv, up_send, up_recv, down_send, down_recv,
     half_send, half_recv, hup_send, hup_recv, hdown_send, hdown_recv, part_send, part_recv,
@@ -86,6 +87,12 @@
             device_id=target, device_id_type=MESH,
         )
 
+    def x_part(i):
+        rows = pl.ds(pl.multiple_of(i * X_PART, X_PART), X_PART)
+        return pltpu.make_async_copy(x_hbm.at[rows], x_ref.at[rows], x_sem.at[i])
+
+    for i in range(ROWS // X_PART):
+        x_part(i).start()
     barrier = pltpu.get_barrier_semaphore()
 
     def greet(d, _):
@@ -109,34 +116,34 @@
     lax.fori_loop(1, NZ, greet_line, 0)
 
     def widen(i, _):
-        part = x_ref[pl.ds(pl.multiple_of(i * 64, 64), 64), :]
-        for f in range(4):
-            wide[pl.ds(pl.multiple_of(i * 64, 64), 64), f, :] = part[:, f * LANES : (f + 1) * LANES].astype(
-                jnp.float32
-            )
+        x_part(i).wait()
+        for j in range(0, X_PART, 64):
+            rows = pl.ds(pl.multiple_of(i * X_PART + j, 64), 64)
+            for f in range(4):
+                wide[f, rows, :] = x_ref[rows, f * LANES : (f + 1) * LANES].astype(jnp.float32)
         return 0
 
-    lax.fori_loop(0, ROWS // 64, widen, 0)
+    lax.fori_loop(0, ROWS // X_PART, widen, 0)
 
     def gather(q):
         plane = (z + FAR_FIRST[q] + NZ) % NZ
 
         def pick(yc, _):
-            base = pl.multiple_of(yc * CAP * 4, 4)
-            for first in range(0, CAP, 16):
-                got = [
-                    wide[source_ref[yc * NZ + plane, first + k]]
-                    for k in range(16)
-                ]
-                for k in range(16):
-                    picked[pl.ds(base + (first + k) * 4, 4), :] = got[k]
+            base = pl.multiple_of(yc * CAP, 8)
+            for first in range(0, CAP, 8):
+                rows = [source_ref[yc * NZ + plane, first + k] for k in range(8)]
+                got = [[wide[f, row] for f in range(4)] for row in rows]
+                for k in range(8):
+                    for f in range(4):
+                        picked[f, base + first + k] = got[k][f]
             return 0
 
         lax.fori_loop(0, 8, pick, 0)
 
         def narrow(yc, _):
             for f in range(4):
-                send[q, f, yc] = picked[pl.ds(yc * CAP * 4 + f, CAP, stride=4), :].astype(jnp.bfloat16)
+                rows = picked[f, pl.ds(pl.multiple_of(yc * CAP, 8), CAP), :]
+                send[q, f, yc] = rows.astype(jnp.bfloat16)
             return 0
 
         lax.fori_loop(0, 8, narrow, 0)
@@ -167,8 +174,8 @@
         copy_to(target, key_ref.at[target[0] * 2 + target[2]], keys_in.at[d], key_send, key_recv).start()
         return 0
 
+    start_rows(0)
     lax.fori_loop(1, PLANE, send_keys, 0)
-    start_rows(0)
     keys_in[0] = key_ref[mine]
     gather(1)
     start_rows(1)
@@ -199,14 +206,16 @@
     half_copy.start()
 
     all_keys = copy_to(peer(1), keys_in.at[pl.ds(1, PLANE - 1)], keys_in.at[pl.ds(1, PLANE - 1)], key_send, key_recv)
-    all_keys.wait_recv()
-    lane = lax.broadcasted_iota(jnp.int32, (NZ, LANES), 1)
-    for m in range(PLANE // 4):
-        k0, k1, k2, k3 = (keys_in[4 * m + i] for i in range(4))
-        k1, k2, k3 = pltpu.roll(k1, 96, 1), pltpu.roll(k2, 64, 1), pltpu.roll(k3, 32, 1)
-        packed[3 * m] = jnp.where(lane < 96, k0, k1)
-        packed[3 * m + 1] = jnp.where(lane < 64, k1, k2)
-        packed[3 * m + 2] = jnp.where(lane < 32, k2, k3)
+
+    def pack_keys():
+        all_keys.wait_recv()
+        lane = lax.broadcasted_iota(jnp.int32, (NZ, LANES), 1)
+        for m in range(PLANE // 4):
+            k0, k1, k2, k3 = (keys_in[4 * m + i] for i in range(4))
+            k1, k2, k3 = pltpu.roll(k1, 96, 1), pltpu.roll(k2, 64, 1), pltpu.roll(k3, 32, 1)
+            packed[3 * m] = jnp.where(lane < 96, k0, k1)
+            packed[3 * m + 1] = jnp.where(lane < 64, k1, k2)
+            packed[3 * m + 2] = jnp.where(lane < 32, k2, k3)
 
     block = 768
     tiles = block // LANES
@@ -326,26 +335,8 @@
         lax.fori_loop(1, 16, lambda d, _: (sheet_from(d).wait_recv(), 0)[1], 0)
         twin_copy(c).start()
 
-    ahead = {
-        0: heavy_far,
-        1: lambda: heavy_on(2),
-        2: heavy_plane,
-        5: heavy_join,
-    }
-    behind = {
-        0: lambda: heavy_on(3),
-        1: lambda: heavy_on(1),
-        6: heavy_sheet,
-        7: heavy_twin,
-    }
-
-    for q, r in enumerate(FAR_FIRST):
-        if q in ahead:
-            ahead[q]()
-        if q + 2 < len(FAR_FIRST):
-            gather(q + 2)
-            start_rows(q + 2)
-        add_up(q)
+    def chain(q):
+        r = FAR_FIRST[q]
         if r == 4:
             up_copy(q, 4, low).start()
             down_copy(q, 4, high).start()
@@ -364,8 +355,45 @@
             down_copy(0, 1, whole).wait_recv()
             total = acc[q] + up_in[0] + down_in[0]
             out_ref[...] = (total * dims_ref[...].astype(jnp.float32)).astype(jnp.bfloat16)
-        if q in behind:
-            behind[q]()
+
+    def issue(q):
+        gather(q)
+        start_rows(q)
+
+    issue(2)
+    heavy_far()
+    gather(3)
+    heavy_on(3)
+    pack_keys()
+    add_up(0)
+    heavy_on(2)
+    start_rows(3)
+    add_up(1)
+    heavy_on(1)
+    chain(0)
+    gather(4)
+    heavy_plane()
+    start_rows(4)
+    add_up(2)
+    chain(1)
+    chain(2)
+    gather(5)
+    heavy_join()
+    start_rows(5)
+    add_up(3)
+    issue(6)
+    add_up(4)
+    chain(3)
+    chain(4)
+    issue(7)
+    heavy_sheet()
+    add_up(5)
+    chain(5)
+    add_up(6)
+    chain(6)
+    add_up(7)
+    heavy_twin()
+    chain(7)
 
     twin_copy(1 - c).wait_recv()
     twin_copy(c).wait_send()
@@ -389,15 +417,20 @@
     f32 = jnp.float32
     return pl.pallas_call(
         fused_kernel,
-        in_specs=[pl.BlockSpec(memory_space=pltpu.SMEM)] + [vmem] * 6,
+        in_specs=[pl.BlockSpec(memory_space=pltpu.SMEM)]
+        + [vmem] * 3
+        + [pl.BlockSpec(memory_space=pl.ANY)]
+        + [vmem] * 2,
         out_specs=(vmem, vmem),
         out_shape=(
             jax.ShapeDtypeStruct((SLOTS, LANES), jnp.bfloat16),
             jax.ShapeDtypeStruct((NY, NZ, NC, NX, 4, F), jnp.bfloat16),
         ),
         scratch_shapes=[
-            pltpu.VMEM((ROWS, 4, LANES), f32),
-            pltpu.VMEM((8 * CAP * 4, LANES), f32),
+            pltpu.VMEM((ROWS, F), jnp.bfloat16),
+            dma((ROWS // X_PART,)),
+            pltpu.VMEM((4, ROWS, LANES), f32),
+            pltpu.VMEM((4, 8 * CAP, LANES), f32),
             pltpu.VMEM((NZ, NX, 8, CAP, LANES), jnp.bfloat16),
             pltpu.VMEM((NZ, PLANE * CAP, LANES), jnp.bfloat16),
             pltpu.VMEM((PLANE, NZ, LANES), jnp.int32),

time: 124 us -> 106 us (0.85)
  Pallas kernels: 120 us -> 101 us
    pallas_call x1, Pallas kernels: 116 us -> 97.1 us  [join(): pl.pallas_call(fused_kernel, in_specs=[pl.BlockSpec(memory_space=pltpu.SM...]
where the time goes in v4:
time: 106 us
  Pallas kernels  101 us (95%)
  local copies, waits for them, and re-layouts  3.81 us (4%)
    pallas_call x1, Pallas kernels, join(): pl.pallas_call(fused_kernel, in_specs=[pl.BlockSpec(memory_space=pltpu.SM...  97.1 us
    pallas_call x1, Pallas kernels, tables(): pl.pallas_call(table_kernel, out_shape=(shape, shape), name='tables')  4.18 us
    reshape x1, local copies, waits for them, and re-layouts, shards(): return (light_joined, heavy_joined.reshape(H, F))  2.14 us

profile of v4, /device:TPU:1, one launch (start us, length us, event | category | flops | bytes accessed | tf_op | source)
XLA Modules:
  0.0 105.7 jit_solution(8820126478165943313)
XLA Ops:
  0.6 4.2 %tables.1 = (s32[64,128]{1,0:T(8,128)}, s32[64,128]{1,0:T(8,128)}) custom-call(s32[32,128]{1,0:T(8,128)} %bitcast.9, s32[32,128]{1,0:T(8,128)} %bitcast.10, s32[32,128]{1,0:T(8,128)} %bitcast.5), custom_call_target="tpu_custom_call" | custom-call | tf_op jit(solution)/shard_map/tables/pallas_call | solution.py:65
  4.8 97.1 %join.1 = (bf16[1024,128]{1,0:T(8,128)(2,1)}, bf16[4,8,2,4,4,512]{5,4,3,2,1,0:T(4,128)(2,1)}) custom-call(s32[64,128]{1,0:T(8,128)} %get-tuple-element.6.source_ref, s32[8,8,128]{2,1,0:T(8,128)} %bitcast.7, s32[32,128]{1,0:T(8,128)} %bitcast.8, s32[32,128]{1,0:T(8,128)} %bitcast.6, bf16[4096,512]{1,0:T(8,128)(2,1)} %x_hbm.1, bf16[1024,128]{1,0:T(8,128)(2,1)} %dims_ref.1, ...), custom_call_target="tpu_custom_call" | custom-call | tf_op jit(solution)/shard_map/join/pallas_call | solution.py:418
  101.9 2.1 %reshape.27 = bf16[1024,512]{1,0:T(8,128)(2,1)} reshape(bf16[4,8,2,4,4,512]{5,4,3,2,1,0:T(4,128)(2,1)} %get-tuple-element.9) | data formatting | bytes 2097152 | tf_op jit(solution)/shard_map/reshape | solution.py:465
  104.1 1.7 %copy.10 = bf16[1024,128]{1,0:T(8,128)(2,1)} copy(bf16[1024,128]{1,0:T(8,128)(2,1)} %get-tuple-element.12) | data formatting | bytes 524288

commit v5 on v4

--- a/solution.py
+++ b/solution.py
@@ -25,7 +25,7 @@
 X_PART = 256
 
 
-def table_kernel(owner_ref, slot_ref, flag_ref, source_ref, key_ref):
+def table_kernel(owner_ref, slot_ref, flag_ref, source_ref, key_ref, hots, ranks):
     K = 2 * LANES
     row = lax.broadcasted_iota(jnp.int32, (K, K), 0)
     col = lax.broadcasted_iota(jnp.int32, (K, K), 1)
@@ -33,27 +33,33 @@
     owner_of = lax.broadcasted_iota(jnp.int32, (OWNERS, K), 0)
     rank_of = lax.broadcasted_iota(jnp.int32, (CAP, K), 0).astype(jnp.float32)
     lane = lax.broadcasted_iota(jnp.int32, (1, K), 1)
-    ones = jnp.ones((K, LANES), jnp.bfloat16)
     seen = jnp.zeros((OWNERS, 1), jnp.float32)
     table = jnp.zeros((4 * CAP, OWNERS), jnp.float32)
+
+    def two(ref, b):
+        return jnp.concatenate([ref[2 * b : 2 * b + 1, :], ref[2 * b + 1 : 2 * b + 2, :]], axis=1)
+
     for b in range(ROWS // K):
-        owner, slot, flag = (
-            jnp.concatenate([ref[2 * b : 2 * b + 1, :], ref[2 * b + 1 : 2 * b + 2, :]], axis=1)
-            for ref in (owner_ref, slot_ref, flag_ref)
-        )
+        owner = two(owner_ref, b)
         owner = (owner >> 4) * 16 + (owner & 1) * 8 + ((owner >> 1) & 7)
-        owner = jnp.where(flag == 0, owner, -1)
+        owner = jnp.where(two(flag_ref, b) == 0, owner, -1)
         hot = jnp.where(owner_of == owner, 1.0, 0.0)
-        hot16 = hot.astype(jnp.bfloat16)
-        counts = jnp.dot(hot16, before, preferred_element_type=jnp.float32)
-        rank = jnp.sum(hot * (counts + seen), axis=0, keepdims=True)
+        hots[b] = hot.astype(jnp.bfloat16)
+        counts = jnp.dot(hots[b], before, preferred_element_type=jnp.float32)
+        ranks[b : b + 1, :] = jnp.sum(hot * (counts + seen), axis=0, keepdims=True)
         seen = seen + jnp.sum(hot, axis=1, keepdims=True)
-        at_rank = rank_of == rank
+    for b in range(ROWS // K):
+        slot = two(slot_ref, b)
+        at_rank = rank_of == ranks[b : b + 1, :]
         high = lax.shift_right_logical(slot, 8)
         values = ((lane & 127) + 1, 2 * b + (lane >> 7), slot - high * 256, high)
         placed = jnp.concatenate(
-            [jnp.where(at_rank, value.astype(jnp.float32), 0.0).astype(jnp.bfloat16) for value in values], axis=0)
-        table = table + lax.dot_general(placed, hot16, (((1,), (1,)), ((), ())), preferred_element_type=jnp.float32)
+            [jnp.where(at_rank, value.astype(jnp.float32), 0.0).astype(jnp.bfloat16) for value in values],
+            axis=0,
+        )
+        table = table + lax.dot_general(
+            placed, hots[b], (((1,), (1,)), ((), ())), preferred_element_type=jnp.float32
+        )
     first, block, low, high = (
         jnp.concatenate([table[i * CAP : (i + 1) * CAP], jnp.zeros((LANES - CAP, OWNERS), jnp.float32)], axis=0).T.astype(jnp.int32) for i in range(4))
     filled = first > 0
@@ -62,12 +68,16 @@
 
 def tables(owner, slot, flag):
     shape = jax.ShapeDtypeStruct((OWNERS, LANES), jnp.int32)
-    return pl.pallas_call(table_kernel, out_shape=(shape, shape), name="tables")(owner, slot, flag)
+    return pl.pallas_call(table_kernel, out_shape=(shape, shape), name="tables",
+        scratch_shapes=[
+            pltpu.VMEM((ROWS // 256, OWNERS, 256), jnp.bfloat16),
+            pltpu.VMEM((ROWS // 256, 256), jnp.float32),
+        ])(owner, slot, flag)
 
 
 def fused_kernel(
-    source_ref, key_ref, hkey_ref, flag_ref, x_hbm, dims_ref, hdims_ref, out_ref, hout,
-    x_ref, x_sem, wide, picked, send, recv, keys_in, packed, up_in, down_in, acc,
+    source_ref, key_hbm, hkey_hbm, flag_hbm, x_hbm, dims_hbm, hdims_hbm, out_ref, hfin_ref,
+    key_ref, hkey_ref, flag_ref, dims_ref, hdims_ref, in_sem, hout, x_ref, x_sem, wide, picked, send, recv, keys_in, packed, up_in, down_in, acc,
     hacc, half_in, hrun, hup_in, hdown_in, hpart, plane_in,
     key_send, key_recv, row_send, row_recv, up_send, up_recv, down_send, down_recv,
     half_send, half_recv, hup_send, hup_recv, hdown_send, hdown_recv, part_send, part_recv,
@@ -77,7 +87,10 @@
     mine = y * 2 + c
 
     def peer(d):
-        return ((y + d // 2 % 4) % 4, z, (c + d % 2) % 2, (x + d // 8) % 4)
+        return (
+            lax.rem(y + lax.rem(lax.div(d, 2), 4), 4), z,
+            lax.rem(c + lax.rem(d, 2), 2), lax.rem(x + lax.div(d, 8), 4),
+        )
 
     up, down = (y, (z + 1) % NZ, c, x), (y, (z + NZ - 1) % NZ, c, x)
 
@@ -95,12 +108,6 @@
         x_part(i).start()
     barrier = pltpu.get_barrier_semaphore()
 
-    def greet(d, _):
-        pl.semaphore_signal(barrier, inc=1, device_id=peer(d), device_id_type=MESH)
-        return 0
-
-    lax.fori_loop(1, PLANE, greet, 0)
-
     def along(d):
         return (y, (z + d) % NZ, c, x)
 
@@ -109,11 +116,33 @@
 
     twin = (y, z, 1 - c, x)
 
-    def greet_line(d, _):
-        pl.semaphore_signal(barrier, inc=1, device_id=along(d), device_id_type=MESH)
-        return 0
-
-    lax.fori_loop(1, NZ, greet_line, 0)
+    ys, xs, cs = (
+        [lax.rem(at + i, count) for i in range(count)] for at, count in ((y, NY), (x, NX), (c, NC))
+    )
+    for dx in (2, 1, 3, 0):
+        for dy in (2, 1, 3, 0):
+            for dc in range(NC):
+                if dx or dy or dc:
+                    pl.semaphore_signal(
+                        barrier, inc=1, device_id=(ys[dy], z, cs[dc], xs[dx]), device_id_type=MESH
+                    )
+    for dz in (4, 3, 5, 2, 6, 1, 7):
+        pl.semaphore_signal(barrier, inc=1, device_id=along(dz), device_id_type=MESH)
+
+    small = [
+        pltpu.make_async_copy(src, dst, in_sem.at[i])
+        for i, (src, dst) in enumerate(
+            (
+                (key_hbm, key_ref),
+                (hkey_hbm, hkey_ref),
+                (flag_hbm, flag_ref),
+                (dims_hbm, dims_ref),
+                (hdims_hbm, hdims_ref),
+            )
+        )
+    ]
+    for copy in small:
+        copy.start()
 
     def widen(i, _):
         x_part(i).wait()
@@ -167,6 +196,8 @@
         return copy_to(peer(1), rest, rest, row_send.at[q], row_recv.at[q])
 
     gather(0)
+    for copy in small:
+        copy.wait()
     pl.semaphore_wait(barrier, PLANE + NZ - 2)
 
     def send_keys(d, _):
@@ -241,6 +272,28 @@
 
         lax.fori_loop(1, PLANE * CAP // block, step, 0)
 
+    half_of = lax.broadcasted_iota(jnp.int32, (HALF, block), 0)
+
+    def add_up_half(q, start):
+        plane = (z + FAR_FIRST[q] + NZ) % NZ
+        keys = pl.ds(start, HALF)
+
+        def part(k):
+            lanes = jnp.concatenate(
+                [packed[k * tiles + i, pl.ds(plane, 1), :] for i in range(tiles)], axis=1
+            )
+            hot = jnp.where(half_of == lanes - start, 1.0, 0.0).astype(jnp.bfloat16)
+            rows = recv[q, pl.ds(pl.multiple_of(k * block, block), block), :]
+            return jnp.dot(hot, rows, preferred_element_type=jnp.float32)
+
+        acc[q, keys, :] = part(0) + down_in[-FAR_FIRST[q], keys, :]
+
+        def step(k, _):
+            acc[q, keys, :] += part(k)
+            return 0
+
+        lax.fori_loop(1, PLANE * CAP // block, step, 0)
+
     low, high, whole = pl.ds(0, HALF), pl.ds(HALF, HALF), pl.ds(0, SLOTS)
 
     def up_copy(q, r, part):
@@ -334,6 +387,15 @@
     def heavy_twin():
         lax.fori_loop(1, 16, lambda d, _: (sheet_from(d).wait_recv(), 0)[1], 0)
         twin_copy(c).start()
+
+    def lay_out(core):
+        def line(i, _):
+            spot = hacc.at[pl.ds(pl.multiple_of((i * 2 + core) * 16, 16), 16)]
+            for j in range(NX):
+                spot[4 * j : 4 * j + 4, :] = hout[i // NZ, i % NZ, core, j].astype(jnp.float32)
+            return 0
+
+        lax.fori_loop(0, NY * NZ, line, 0)
 
     def chain(q):
         r = FAR_FIRST[q]
@@ -389,15 +451,21 @@
     heavy_sheet()
     add_up(5)
     chain(5)
-    add_up(6)
-    chain(6)
+    down_copy(0, 2, whole).wait_recv()
+    rows_of(6).wait_recv()
+    for keys in (low, high):
+        add_up_half(6, keys.start)
+        down_copy(6, 1, keys).start()
     add_up(7)
     heavy_twin()
+    half_copy.wait_send()
+    lay_out(c)
     chain(7)
 
     twin_copy(1 - c).wait_recv()
+    lay_out(1 - c)
+    hfin_ref[...] = hacc[...].astype(jnp.bfloat16)
     twin_copy(c).wait_send()
-    half_copy.wait_send()
     lax.fori_loop(1, 16, lambda d, _: (part_copy(d).wait_send(), 0)[1], 0)
     lax.fori_loop(1, 16, lambda d, _: (sheet_copy(d).wait_send(), 0)[1], 0)
     lax.fori_loop(1, NZ, lambda d, _: (line_copy(d).wait_send(), 0)[1], 0)
@@ -418,15 +486,20 @@
     return pl.pallas_call(
         fused_kernel,
         in_specs=[pl.BlockSpec(memory_space=pltpu.SMEM)]
-        + [vmem] * 3
-        + [pl.BlockSpec(memory_space=pl.ANY)]
-        + [vmem] * 2,
+        + [pl.BlockSpec(memory_space=pl.ANY)] * 6,
         out_specs=(vmem, vmem),
         out_shape=(
             jax.ShapeDtypeStruct((SLOTS, LANES), jnp.bfloat16),
-            jax.ShapeDtypeStruct((NY, NZ, NC, NX, 4, F), jnp.bfloat16),
+            jax.ShapeDtypeStruct((H, F), jnp.bfloat16),
         ),
         scratch_shapes=[
+            pltpu.VMEM((8, NZ, LANES), jnp.int32),
+            pltpu.VMEM((ROWS // LANES, LANES), jnp.int32),
+            pltpu.VMEM((ROWS // LANES, LANES), jnp.int32),
+            pltpu.VMEM((SLOTS, LANES), jnp.bfloat16),
+            pltpu.VMEM((4, F), jnp.bfloat16),
+            dma((5,)),
+            pltpu.VMEM((NY, NZ, NC, NX, 4, F), jnp.bfloat16),
             pltpu.VMEM((ROWS, F), jnp.bfloat16),
             dma((ROWS // X_PART,)),
             pltpu.VMEM((4, ROWS, LANES), f32),
@@ -456,13 +529,47 @@
     )(source, key.reshape(8, NZ, LANES), heavy_key, flag, rows, light_dims, heavy_dims)
 
 
+def keep_kernel(light_in, heavy_in, light_out, heavy_out, light, heavy, came, gone):
+    quarter = H // 4
+    spans = [pl.ds(i * quarter, quarter) for i in range(4)]
+    moves = [(light_in, light, light_out)] + [
+        (heavy_in.at[rows], heavy.at[rows], heavy_out.at[rows]) for rows in spans
+    ]
+    ins = [pltpu.make_async_copy(a, b, came.at[i]) for i, (a, b, _) in enumerate(moves)]
+    outs = [pltpu.make_async_copy(b, c, gone.at[i]) for i, (_, b, c) in enumerate(moves)]
+    for copy in ins:
+        copy.start()
+    for arrives, leaves in zip(ins, outs):
+        arrives.wait()
+        leaves.start()
+    for copy in outs:
+        copy.wait()
+
+
+def keep(light, heavy):
+    anywhere = pl.BlockSpec(memory_space=pl.ANY)
+    return pl.pallas_call(
+        keep_kernel,
+        in_specs=[anywhere] * 2,
+        out_specs=(anywhere, anywhere),
+        out_shape=tuple(jax.ShapeDtypeStruct(v.shape, v.dtype) for v in (light, heavy)),
+        scratch_shapes=[
+            pltpu.VMEM(light.shape, light.dtype),
+            pltpu.VMEM(heavy.shape, heavy.dtype),
+            pltpu.SemaphoreType.DMA((5,)),
+            pltpu.SemaphoreType.DMA((5,)),
+        ],
+        name="keep",
+    )(light, heavy)
+
+
 def shards(rows, owner, slot, flag, heavy_key, light_dims, heavy_dims):
     owner, slot, flag, heavy_key = (
         v.reshape(ROWS // LANES, LANES) for v in (owner, slot, flag, heavy_key)
     )
     source, key = tables(owner, slot, flag)
     light_joined, heavy_joined = join(source, key, heavy_key, flag, rows, light_dims, heavy_dims)
-    return light_joined, heavy_joined.reshape(H, F)
+    return keep(light_joined, heavy_joined)
 
 
 def solution(mesh):

time: 106 us -> 103 us (0.972)
  local copies, waits for them, and re-layouts: 3.81 us -> 0 us
    reshape x1 -> x0, local copies, waits for them, and re-layouts: 2.14 us -> none  [shards(): return (light_joined, heavy_joined.reshape(H, F))]
    unnamed x1 -> x0, local copies, waits for them, and re-layouts: 1.67 us -> none
    pallas_call x1 -> x2, Pallas kernels: 4.18 us -> 4.93 us  [the longest x1 2.85 us: tables(): pl.pallas_call(table_kernel, out_shape=(shape, shape), name='tables', scr...]
where the time goes in v5:
time: 103 us; the launch traced here: 102 us
  Pallas kernels  102 us (99%)
    pallas_call x1, Pallas kernels, join(): pl.pallas_call(fused_kernel, in_specs=[pl.BlockSpec(memory_space=pltpu.SM...  96.8 us
    pallas_call x1, Pallas kernels, tables(): pl.pallas_call(table_kernel, out_shape=(shape, shape), name='tables', scr...  2.85 us
    pallas_call x1, Pallas kernels, keep(): pl.pallas_call(keep_kernel, in_specs=[anywhere] * 2, out_specs=(anywhere,...  2.08 us

profile of v5, /device:TPU:1, one launch (start us, length us, event | category | flops | bytes accessed | tf_op | source)
XLA Modules:
  0.0 102.3 jit_solution(4988881932967922740)
XLA Ops:
  0.6 2.8 %tables.1 = (s32[64,128]{1,0:T(8,128)}, s32[64,128]{1,0:T(8,128)}) custom-call(s32[32,128]{1,0:T(8,128)} %bitcast.9, s32[32,128]{1,0:T(8,128)} %bitcast.10, s32[32,128]{1,0:T(8,128)} %bitcast.5), custom_call_target="tpu_custom_call" | custom-call | tf_op jit(solution)/shard_map/tables/pallas_call | solution.py:71
  3.5 96.8 %join.1 = (bf16[1024,128]{1,0:T(8,128)(2,1)}, bf16[1024,512]{1,0:T(8,128)(2,1)}) custom-call(s32[64,128]{1,0:T(8,128)} %get-tuple-element.6.source_ref, s32[8,8,128]{2,1,0:T(8,128)} %bitcast.7, s32[32,128]{1,0:T(8,128)} %bitcast.8, s32[32,128]{1,0:T(8,128)} %bitcast.6, bf16[4096,512]{1,0:T(8,128)(2,1)} %x_hbm.1, bf16[1024,128]{1,0:T(8,128)(2,1)} %dims_hbm.1, ...), custom_call_target="tpu_custom_call" | custom-call | tf_op jit(solution)/shard_map/join/pallas_call | solution.py:486
  100.3 2.1 %keep.1 = (bf16[1024,128]{1,0:T(8,128)(2,1)}, bf16[1024,512]{1,0:T(8,128)(2,1)}) custom-call(bf16[1024,128]{1,0:T(8,128)(2,1)} %get-tuple-element.8.light_in, bf16[1024,512]{1,0:T(8,128)(2,1)} %get-tuple-element.9.heavy_in), custom_call_target="tpu_custom_call" | custom-call | tf_op jit(solution)/shard_map/keep/pallas_call | solution.py:551
